TPU v7x, 32 devices: a whole 2x2x4 slice. The times are simulated.
32 devices in a mesh: cp: 8 (over z, x), tp: 4 (over y, core).
Axes of the slice: x: 2, y: 2, z: 4, core: 2. Of those that a mesh axis runs over, the one named last changes fastest.
Arguments:
- tokens_in: bfloat16 [2048, 2048], P('cp'), may hold values from -6 to 6
- doc_ids: int32 [2048], P('cp'), may hold values from 0 to 3, never falling along the last dimension, each value on 1 to 1024 neighbouring positions
- expert_ids: int32 [2048, 2], P('cp'), may hold values from 0 to 7, all different within a row; in each aligned block of 256 rows (0 to 255, 256 to 511, ...) at most 96 rows name the same one
- attn_gain: bfloat16 [2048], P('cp'), may hold values from 0.099609375 to 1.8984375
- q_gain: bfloat16 [128], replicated, may hold values from 0.099609375 to 1.8984375
- k_gain: bfloat16 [128], replicated, may hold values from 0.099609375 to 1.8984375
- w_query: bfloat16 [2048, 2048], P('cp', 'tp'), may hold values from -0.125 to 0.125
- w_key: bfloat16 [2048, 2048], P('cp', 'tp'), may hold values from -0.125 to 0.125
- w_value: bfloat16 [2048, 2048], P('cp', 'tp'), may hold values from -0.125 to 0.125
- w_output: bfloat16 [2048, 2048], P('cp', 'tp'), may hold values from -2 to 2
- ffn_gain: bfloat16 [2048], P('cp'), may hold values from 0.099609375 to 1.8984375
- w_router: bfloat16 [2048, 8], P('cp'), may hold values from -0.25 to 0.25
- w_gate: bfloat16 [2048, 8, 1024], P('cp', None, 'tp'), may hold values from -0.125 to 0.125
- w_up: bfloat16 [2048, 8, 1024], P('cp', None, 'tp'), may hold values from -0.125 to 0.125
- w_down: bfloat16 [2048, 8, 1024], P('cp', None, 'tp'), may hold values from -0.75 to 0.75
- cotangent: bfloat16 [2048, 2048], P('cp'), may hold values from -6 to 6
Outputs:
- block_out: bfloat16 [2048, 2048], P('cp')
- grad_in: float32 [2048, 2048], P('cp')
- grad_attn_gain: float32 [2048], P('cp')
- grad_q_gain: float32 [128], replicated
- grad_k_gain: float32 [128], replicated
- grad_query: float32 [2048, 2048], P('cp', 'tp')
- grad_key: float32 [2048, 2048], P('cp', 'tp')
- grad_value: float32 [2048, 2048], P('cp', 'tp')
- grad_output: float32 [2048, 2048], P('cp', 'tp')
- grad_ffn_gain: float32 [2048], P('cp')
- grad_router: float32 [2048, 8], P('cp')
- grad_gate: float32 [2048, 8, 1024], P('cp', None, 'tp')
- grad_up: float32 [2048, 8, 1024], P('cp', None, 'tp')
- grad_down: float32 [2048, 8, 1024], P('cp', None, 'tp')
Inputs may be any that keep to these rules, and one draw needn't show every extreme that they name: `doc_ids`: document numbers never fall along the stream; every document holds 1 to 1024 tokens and one holds exactly 1024. `expert_ids`: the 2 experts of a token differ. Among the tokens of one index of cp no expert is named more than 96 times, and on some index some expert is named exactly 96 times.
All inputs are finite; a program needn't handle non-finite values.
Results may differ from a plain program's by a relative error of at most 0.025.
Values may be sent and summed in bfloat16 or wider, within the bound.
A program may use at most 256 MiB of HBM per device.

v0:
```python
import jax
import jax.numpy as jnp
from jax import lax
from jax.sharding import PartitionSpec as P

CAP = 96


eps = 1e-05
theta = 50000.0
negative = -1e30


def rms_norm(values, gain_vec):
    factor = lax.rsqrt(jnp.mean(values * values, axis=-1, keepdims=True) + eps)
    return values * factor * gain_vec


def rotary_tables(positions, head_dim):
    half_dim = head_dim // 2
    inverse_freq = theta ** (-2.0 * jnp.arange(half_dim, dtype=jnp.float32) / head_dim)
    angles = positions[:, None] * inverse_freq[None, :]
    cos_tab = jnp.concatenate([jnp.cos(angles), jnp.cos(angles)], axis=-1)
    sin_tab = jnp.concatenate([jnp.sin(angles), jnp.sin(angles)], axis=-1)
    return (cos_tab, sin_tab)


def rotate_half(tensor):
    half_dim = tensor.shape[-1] // 2
    return jnp.concatenate([-tensor[..., half_dim:], tensor[..., :half_dim]], axis=-1)


def qk_prepare(raw_heads, gain_vec, cos_tab, sin_tab):
    normed = rms_norm(raw_heads, gain_vec)
    return normed * cos_tab[:, None, :] + rotate_half(normed) * sin_tab[:, None, :]


def gather_attention(w_query, w_key, w_value, w_output, attn_gain):
    return (
        lax.all_gather(w_query, "cp", axis=0, tiled=True),
        lax.all_gather(w_key, "cp", axis=0, tiled=True),
        lax.all_gather(w_value, "cp", axis=0, tiled=True),
        lax.all_gather(w_output, "cp", axis=0, tiled=True),
        lax.all_gather(attn_gain, "cp", axis=0, tiled=True),
    )


def gather_experts(w_gate, w_up, w_down, w_router, ffn_gain):
    return (
        lax.all_gather(w_gate, "cp", axis=0, tiled=True),
        lax.all_gather(w_up, "cp", axis=0, tiled=True),
        lax.all_gather(w_down, "cp", axis=0, tiled=True),
        lax.all_gather(w_router, "cp", axis=0, tiled=True),
        lax.all_gather(ffn_gain, "cp", axis=0, tiled=True),
    )


def gather_keys(k_flat, v_low):
    return (
        lax.all_gather(k_flat, "cp", axis=0, tiled=True),
        lax.all_gather(v_low, "cp", axis=0, tiled=True),
    )


def block_scores(q_rot, key_block, local_docs, doc_block, scale_factor):
    scores = (
        jnp.einsum("qhd,khd->hqk", q_rot, key_block, preferred_element_type=jnp.float32)
        * scale_factor
    )
    keep_mask = (local_docs[:, None] == doc_block[None, :])[None, :, :]
    return (scores, keep_mask)


def visit(step_fn, carry, source):
    keys, values, docs = source

    def scan_step(running, inputs):
        return (step_fn(running, inputs[0], inputs[1], inputs[2]), None)

    result, unused = lax.scan(scan_step, carry, (keys, values, docs))
    return result


def attention_forward(q_rot, source, local_docs, scale_factor):
    tok_rows, heads_local, head_dim = q_rot.shape

    def norm_step(running, key_block, value_block, doc_block):
        run_max, run_sum = running
        scores, keep_mask = block_scores(q_rot, key_block, local_docs, doc_block, scale_factor)
        new_max = jnp.maximum(run_max, jnp.max(jnp.where(keep_mask, scores, negative), axis=-1))
        terms = jnp.where(keep_mask, jnp.exp(scores - new_max[:, :, None]), 0.0)
        return (new_max, run_sum * jnp.exp(run_max - new_max) + jnp.sum(terms, axis=-1))

    start_max = jnp.full((heads_local, tok_rows), negative, jnp.float32)
    start_sum = jnp.zeros((heads_local, tok_rows), jnp.float32)
    run_max, run_sum = visit(norm_step, (start_max, start_sum), source)
    log_norm = run_max + jnp.log(run_sum)

    def out_step(running, key_block, value_block, doc_block):
        scores, keep_mask = block_scores(q_rot, key_block, local_docs, doc_block, scale_factor)
        probs_low = jnp.where(keep_mask, jnp.exp(scores - log_norm[:, :, None]), 0.0).astype(
            jnp.bfloat16
        )
        return running + jnp.einsum(
            "hqk,khd->qhd", probs_low, value_block, preferred_element_type=jnp.float32
        )

    start_out = jnp.zeros((tok_rows, heads_local, head_dim), jnp.float32)
    heads_acc = visit(out_step, start_out, source)
    return (log_norm, heads_acc)


def forward_pass(
    tokens, attn_set, expert_set, q_gain, k_gain, cos_tab, sin_tab, local_docs, all_docs, expert_ids
):
    full_query, full_key, full_value, full_output, attn_gain = attn_set
    full_gate, full_up, full_down, full_router, ffn_gain = expert_set
    tok_rows = tokens.shape[0]
    head_dim = q_gain.shape[0]
    head_width = full_query.shape[1]
    heads_local = head_width // head_dim
    scale_factor = head_dim ** (-0.5)
    normed_in = rms_norm(tokens, attn_gain.astype(jnp.float32)).astype(jnp.bfloat16)
    q_raw = jnp.dot(normed_in, full_query, preferred_element_type=jnp.float32).reshape(
        tok_rows, heads_local, head_dim
    )
    k_raw = jnp.dot(normed_in, full_key, preferred_element_type=jnp.float32).reshape(
        tok_rows, heads_local, head_dim
    )
    v_low = jnp.dot(normed_in, full_value, preferred_element_type=jnp.float32).astype(jnp.bfloat16)
    q_rot = qk_prepare(q_raw, q_gain.astype(jnp.float32), cos_tab, sin_tab).astype(jnp.bfloat16)
    k_rot = qk_prepare(k_raw, k_gain.astype(jnp.float32), cos_tab, sin_tab).astype(jnp.bfloat16)
    keys_all, values_all = gather_keys(k_rot.reshape(tok_rows, head_width), v_low)
    stream_len = keys_all.shape[0]
    block_rows = 512
    count_blocks = stream_len // block_rows
    source = (
        keys_all.reshape(count_blocks, block_rows, heads_local, head_dim),
        values_all.reshape(count_blocks, block_rows, heads_local, head_dim),
        all_docs.reshape(count_blocks, block_rows),
    )
    log_norm, heads_acc = attention_forward(q_rot, source, local_docs, scale_factor)
    heads_out = heads_acc.astype(jnp.bfloat16).reshape(tok_rows, head_width)
    attn_part = lax.dot_general(
        heads_out, full_output, (((1,), (1,)), ((), ())), preferred_element_type=jnp.float32
    )
    attn_mix = lax.psum(attn_part, "tp")
    hidden = tokens + attn_mix
    normed_mid = rms_norm(hidden, ffn_gain.astype(jnp.float32)).astype(jnp.bfloat16)
    logits = jnp.dot(normed_mid, full_router, preferred_element_type=jnp.float32)
    router_probs = jax.nn.softmax(logits, axis=-1)
    experts = full_router.shape[1]
    top_count = expert_ids.shape[1]
    picked = expert_ids[:, :, None] == jnp.arange(experts, dtype=jnp.int32)[None, None, :]
    picked_float = picked.astype(jnp.float32)
    picked_int = picked.astype(jnp.int32)
    combine = jnp.sum(router_probs[:, None, :] * picked_float, axis=-1)
    counts = jnp.sum(picked_int, axis=1)
    before = jnp.cumsum(counts, axis=0) - counts
    slot_rank = jnp.sum(before[:, None, :] * picked_int, axis=-1)
    flat_slots = (expert_ids * CAP + slot_rank).reshape(-1)
    slot_total = experts * CAP
    token_index = jnp.repeat(jnp.arange(tok_rows, dtype=jnp.int32), top_count)
    token_of_slot = jnp.zeros((slot_total,), jnp.int32).at[flat_slots].set(token_index)
    weight_of_slot = jnp.zeros((slot_total,), jnp.float32).at[flat_slots].set(combine.reshape(-1))
    slot_inputs = normed_mid[token_of_slot].reshape(experts, CAP, -1)
    gate_pre = jnp.einsum(
        "ecd,def->ecf", slot_inputs, full_gate, preferred_element_type=jnp.float32
    )
    up_pre = jnp.einsum("ecd,def->ecf", slot_inputs, full_up, preferred_element_type=jnp.float32)
    activated = (jax.nn.silu(gate_pre) * up_pre).astype(jnp.bfloat16)
    expert_out = jnp.einsum(
        "ecf,def->ecd", activated, full_down, preferred_element_type=jnp.float32
    )
    picked_out = expert_out.reshape(slot_total, -1)[flat_slots].reshape(tok_rows, top_count, -1)
    mixture_part = jnp.sum(combine[:, :, None] * picked_out, axis=1)
    expert_mix = lax.psum(mixture_part.astype(jnp.bfloat16), "tp").astype(jnp.float32)
    return {
        "output": hidden + expert_mix,
        "normed_in": normed_in,
        "q_raw": q_raw,
        "k_raw": k_raw,
        "q_rot": q_rot,
        "heads_out": heads_out,
        "log_norm": log_norm,
        "source_keys": source[0],
        "source_values": source[1],
        "source_docs": source[2],
        "hidden": hidden,
        "normed_mid": normed_mid,
        "router_probs": router_probs,
        "picked_float": picked_float,
        "flat_slots": flat_slots,
        "token_of_slot": token_of_slot,
        "weight_of_slot": weight_of_slot,
        "slot_inputs": slot_inputs,
        "gate_pre": gate_pre,
        "up_pre": up_pre,
        "activated": activated,
        "expert_out": expert_out,
    }


def on_device(
    tokens_in,
    doc_ids,
    expert_ids,
    attn_gain,
    q_gain,
    k_gain,
    w_query,
    w_key,
    w_value,
    w_output,
    ffn_gain,
    w_router,
    w_gate,
    w_up,
    w_down,
    cotangent,
):
    tok_rows = tokens_in.shape[0]
    head_dim = q_gain.shape[0]
    head_width = w_query.shape[1]
    heads_local = head_width // head_dim
    scale_factor = head_dim ** (-0.5)
    top_count = expert_ids.shape[1]
    positions = (lax.axis_index("cp") * tok_rows + jnp.arange(tok_rows, dtype=jnp.int32)).astype(
        jnp.float32
    )
    cos_tab, sin_tab = rotary_tables(positions, head_dim)
    all_docs = lax.all_gather(doc_ids, "cp", axis=0, tiled=True)
    tokens = tokens_in.astype(jnp.float32)
    attn_set = gather_attention(w_query, w_key, w_value, w_output, attn_gain)
    expert_set = gather_experts(w_gate, w_up, w_down, w_router, ffn_gain)
    stored = forward_pass(
        tokens,
        attn_set,
        expert_set,
        q_gain,
        k_gain,
        cos_tab,
        sin_tab,
        doc_ids,
        all_docs,
        expert_ids,
    )
    block_out = stored["output"].astype(jnp.bfloat16)
    fenced = lax.optimization_barrier(
        (
            block_out,
            w_query,
            w_key,
            w_value,
            w_output,
            attn_gain,
            w_gate,
            w_up,
            w_down,
            w_router,
            ffn_gain,
            tokens,
        )
    )
    attn_set = gather_attention(fenced[1], fenced[2], fenced[3], fenced[4], fenced[5])
    expert_set = gather_experts(fenced[6], fenced[7], fenced[8], fenced[9], fenced[10])
    stored = forward_pass(
        fenced[11],
        attn_set,
        expert_set,
        q_gain,
        k_gain,
        cos_tab,
        sin_tab,
        doc_ids,
        all_docs,
        expert_ids,
    )
    full_query, full_key, full_value, full_output, gathered_attn_gain = attn_set
    full_gate, full_up, full_down, full_router, gathered_ffn_gain = expert_set
    experts = full_router.shape[1]
    slot_total = experts * CAP
    flat_slots = stored["flat_slots"]
    router_probs = stored["router_probs"]
    normed_mid = stored["normed_mid"]
    slot_inputs = stored["slot_inputs"]
    activated = stored["activated"]
    cot_float = cotangent.astype(jnp.float32)
    slot_cot = cotangent[stored["token_of_slot"]].astype(jnp.float32)
    d_expert = (
        (stored["weight_of_slot"][:, None] * slot_cot)
        .astype(jnp.bfloat16)
        .reshape(experts, CAP, -1)
    )
    d_act = jnp.einsum("ecd,def->ecf", d_expert, full_down, preferred_element_type=jnp.float32)
    combine_slot = jnp.sum(
        slot_cot.reshape(experts, CAP, -1) * stored["expert_out"], axis=-1
    ).reshape(-1)
    combine_part = combine_slot[flat_slots].reshape(tok_rows, top_count)
    act_value, act_back = jax.vjp(
        lambda gate_in, up_in: jax.nn.silu(gate_in) * up_in, stored["gate_pre"], stored["up_pre"]
    )
    d_gate, d_up = act_back(d_act)
    d_gate = d_gate.astype(jnp.bfloat16)
    d_up = d_up.astype(jnp.bfloat16)
    d_slots = jnp.einsum(
        "ecf,def->ecd", d_gate, full_gate, preferred_element_type=jnp.float32
    ) + jnp.einsum("ecf,def->ecd", d_up, full_up, preferred_element_type=jnp.float32)
    mid_part = jnp.sum(
        d_slots.reshape(slot_total, -1)[flat_slots].reshape(tok_rows, top_count, -1), axis=1
    )
    mid_sum, d_combine = (
        lax.psum(mid_part.astype(jnp.bfloat16), "tp").astype(jnp.float32),
        lax.psum(combine_part.astype(jnp.bfloat16), "tp").astype(jnp.float32),
    )
    d_probs = jnp.sum(d_combine[:, :, None] * stored["picked_float"], axis=1)
    d_logits = (
        router_probs * (d_probs - jnp.sum(router_probs * d_probs, axis=-1, keepdims=True))
    ).astype(jnp.bfloat16)
    d_mid = mid_sum + lax.dot_general(
        d_logits, full_router, (((1,), (1,)), ((), ())), preferred_element_type=jnp.float32
    )
    mid_value, mid_back = jax.vjp(rms_norm, stored["hidden"], gathered_ffn_gain.astype(jnp.float32))
    d_hidden_norm, ffn_gain_term = mid_back(d_mid)
    d_hidden = cot_float + d_hidden_norm
    router_term = lax.dot_general(
        normed_mid, d_logits, (((0,), (0,)), ((), ())), preferred_element_type=jnp.float32
    )
    q_rot = stored["q_rot"]
    log_norm = stored["log_norm"]
    heads_out = stored["heads_out"]
    source = (stored["source_keys"], stored["source_values"], stored["source_docs"])
    d_attn = d_hidden.astype(jnp.bfloat16)
    d_heads = (
        jnp.dot(d_attn, full_output, preferred_element_type=jnp.float32)
        .astype(jnp.bfloat16)
        .reshape(tok_rows, heads_local, head_dim)
    )

    def delta_step(running, key_block, value_block, doc_block):
        scores, keep_mask = block_scores(q_rot, key_block, doc_ids, doc_block, scale_factor)
        soft_probs = jnp.where(keep_mask, jnp.exp(scores - log_norm[:, :, None]), 0.0)
        d_soft = jnp.einsum(
            "qhd,khd->hqk", d_heads, value_block, preferred_element_type=jnp.float32
        )
        return running + jnp.sum(soft_probs * d_soft, axis=-1)

    row_delta = visit(delta_step, jnp.zeros((heads_local, tok_rows), jnp.float32), source)

    def block_grads(key_block, value_block, doc_block):
        key_rows = key_block.shape[0]
        scores, keep_mask = block_scores(q_rot, key_block, doc_ids, doc_block, scale_factor)
        soft_probs = jnp.where(keep_mask, jnp.exp(scores - log_norm[:, :, None]), 0.0)
        d_soft = jnp.einsum(
            "qhd,khd->hqk", d_heads, value_block, preferred_element_type=jnp.float32
        )
        d_scores = (soft_probs * (d_soft - row_delta[:, :, None])).astype(jnp.bfloat16)
        query_term = scale_factor * jnp.einsum(
            "hqk,khd->qhd", d_scores, key_block, preferred_element_type=jnp.float32
        )
        key_grad = scale_factor * jnp.einsum(
            "hqk,qhd->khd", d_scores, q_rot, preferred_element_type=jnp.float32
        )
        value_grad = jnp.einsum(
            "hqk,qhd->khd",
            soft_probs.astype(jnp.bfloat16),
            d_heads,
            preferred_element_type=jnp.float32,
        )
        return (
            query_term,
            key_grad.reshape(key_rows, head_width),
            value_grad.reshape(key_rows, head_width),
        )

    start_grad = jnp.zeros((tok_rows, heads_local, head_dim), jnp.float32)

    def grad_step(running, inputs):
        query_term, key_grad, value_grad = block_grads(inputs[0], inputs[1], inputs[2])
        return (running + query_term, (key_grad, value_grad))

    d_q_rot, (key_grads, value_grads) = lax.scan(grad_step, start_grad, source)
    stream_len = key_grads.shape[0] * key_grads.shape[1]
    d_k_rot, d_values = (
        lax.psum_scatter(
            key_grads.reshape(stream_len, head_width).astype(jnp.bfloat16),
            "cp",
            scatter_dimension=0,
            tiled=True,
        ).astype(jnp.float32),
        lax.psum_scatter(
            value_grads.reshape(stream_len, head_width).astype(jnp.bfloat16),
            "cp",
            scatter_dimension=0,
            tiled=True,
        ).astype(jnp.float32),
    )
    rotated, q_back = jax.vjp(
        lambda raw_heads, gain_vec: qk_prepare(raw_heads, gain_vec, cos_tab, sin_tab),
        stored["q_raw"],
        q_gain.astype(jnp.float32),
    )
    d_q_raw, q_gain_term = q_back(d_q_rot)
    rotated, k_back = jax.vjp(
        lambda raw_heads, gain_vec: qk_prepare(raw_heads, gain_vec, cos_tab, sin_tab),
        stored["k_raw"],
        k_gain.astype(jnp.float32),
    )
    d_k_raw, k_gain_term = k_back(d_k_rot.reshape(tok_rows, heads_local, head_dim))
    d_q_low = d_q_raw.reshape(tok_rows, head_width).astype(jnp.bfloat16)
    d_k_low = d_k_raw.reshape(tok_rows, head_width).astype(jnp.bfloat16)
    d_v_low = d_values.astype(jnp.bfloat16)
    contract_last = (((1,), (1,)), ((), ()))
    in_part = lax.dot_general(
        d_q_low, full_query, contract_last, preferred_element_type=jnp.float32
    )
    in_part = in_part + lax.dot_general(
        d_k_low, full_key, contract_last, preferred_element_type=jnp.float32
    )
    in_part = in_part + lax.dot_general(
        d_v_low, full_value, contract_last, preferred_element_type=jnp.float32
    )
    d_in_norm = lax.psum(in_part.astype(jnp.bfloat16), "tp").astype(jnp.float32)
    in_value, in_back = jax.vjp(rms_norm, tokens, gathered_attn_gain.astype(jnp.float32))
    d_tokens_norm, attn_gain_term = in_back(d_in_norm)
    grad_in = d_hidden + d_tokens_norm
    normed_in = stored["normed_in"]
    proj_grads = jnp.concatenate([d_q_low, d_k_low, d_v_low], axis=1)
    contract_rows = (((0,), (0,)), ((), ()))
    front_part = lax.dot_general(
        normed_in, proj_grads, contract_rows, preferred_element_type=jnp.float32
    )
    back_part = lax.dot_general(
        d_attn, heads_out, contract_rows, preferred_element_type=jnp.float32
    )
    attention_grads = lax.psum_scatter(
        jnp.concatenate([front_part, back_part], axis=1).astype(jnp.bfloat16),
        "cp",
        scatter_dimension=0,
        tiled=True,
    ).astype(jnp.float32)
    gate_term = jnp.einsum("ecd,ecf->def", slot_inputs, d_gate, preferred_element_type=jnp.float32)
    up_term = jnp.einsum("ecd,ecf->def", slot_inputs, d_up, preferred_element_type=jnp.float32)
    down_term = jnp.einsum("ecd,ecf->def", d_expert, activated, preferred_element_type=jnp.float32)
    expert_grads = lax.psum_scatter(
        jnp.concatenate([gate_term, up_term, down_term], axis=2).astype(jnp.bfloat16),
        "cp",
        scatter_dimension=0,
        tiled=True,
    ).astype(jnp.float32)
    grad_router, grad_attn_gain, grad_ffn_gain = (
        lax.psum_scatter(
            router_term.astype(jnp.bfloat16), "cp", scatter_dimension=0, tiled=True
        ).astype(jnp.float32),
        lax.psum_scatter(
            attn_gain_term.astype(jnp.bfloat16), "cp", scatter_dimension=0, tiled=True
        ).astype(jnp.float32),
        lax.psum_scatter(
            ffn_gain_term.astype(jnp.bfloat16), "cp", scatter_dimension=0, tiled=True
        ).astype(jnp.float32),
    )
    grad_q_gain, grad_k_gain = lax.psum((q_gain_term, k_gain_term), ("cp", "tp"))
    grad_query = attention_grads[:, :head_width]
    grad_key = attention_grads[:, head_width : 2 * head_width]
    grad_value = attention_grads[:, 2 * head_width : 3 * head_width]
    grad_output = attention_grads[:, 3 * head_width :]
    ff_local = w_gate.shape[2]
    grad_gate = expert_grads[:, :, :ff_local]
    grad_up = expert_grads[:, :, ff_local : 2 * ff_local]
    grad_down = expert_grads[:, :, 2 * ff_local :]
    return (
        block_out,
        grad_in,
        grad_attn_gain,
        grad_q_gain,
        grad_k_gain,
        grad_query,
        grad_key,
        grad_value,
        grad_output,
        grad_ffn_gain,
        grad_router,
        grad_gate,
        grad_up,
        grad_down,
    )


def solution(mesh):
    return jax.shard_map(
        on_device,
        mesh=mesh,
        in_specs=(
            P("cp", None),
            P("cp"),
            P("cp", None),
            P("cp"),
            P(),
            P(),
            P("cp", "tp"),
            P("cp", "tp"),
            P("cp", "tp"),
            P("cp", "tp"),
            P("cp"),
            P("cp", None),
            P("cp", None, "tp"),
            P("cp", None, "tp"),
            P("cp", None, "tp"),
            P("cp", None),
        ),
        out_specs=(
            P("cp", None),
            P("cp", None),
            P("cp"),
            P(),
            P(),
            P("cp", "tp"),
            P("cp", "tp"),
            P("cp", "tp"),
            P("cp", "tp"),
            P("cp"),
            P("cp", None),
            P("cp", None, "tp"),
            P("cp", None, "tp"),
            P("cp", None, "tp"),
        ),
        check_vma=False,
    )
```

profile of v0, /device:TPU:0, one launch (start us, length us, event | category | flops | bytes accessed | tf_op | source)
XLA Modules:
  0.0 2523.6 jit_solution(14913780934991762010)
XLA Ops:
  10.1 22.3 all-gather
  34.8 27.3 %all-gather.32.cloned.1.call-done = bf16[2048,512]{1,0:T(8,128)(2,1)} async-done(((bf16[256,512]{1,0:T(8,128)(2,1)}), bf16[2048,512]{1,0:T(8,128)(2,1)}) %all-gather.32.cloned.1.call-update) | async-done | bytes 2097168 | tf_op jit(solution)/shard_map/all_gather | solution.py:40
  65.3 46.6 %all-gather.28.cloned.1.call-done = bf16[2048,512]{1,0:T(8,128)(2,1)} async-done(((bf16[256,512]{1,0:T(8,128)(2,1)}), bf16[2048,512]{1,0:T(8,128)(2,1)}) %all-gather.28.cloned.1.call-update) | async-done | bytes 2097168 | tf_op jit(solution)/shard_map/all_gather | solution.py:41
  120.4 41.2 %all-gather.24.cloned.1.call-done = bf16[2048,512]{1,0:T(8,128)(2,1)} async-done(((bf16[256,512]{1,0:T(8,128)(2,1)}), bf16[2048,512]{1,0:T(8,128)(2,1)}) %all-gather.24.cloned.1.call-update) | async-done | bytes 2097168 | tf_op jit(solution)/shard_map/all_gather | solution.py:42
  165.4 18.3 all-gather.1
  183.9 28.0 %all-gather.30.cloned.1.call-done = bf16[2048,512]{1,0:T(8,128)(2,1)} async-done(((bf16[256,512]{1,0:T(8,128)(2,1)}), bf16[2048,512]{1,0:T(8,128)(2,1)}) %all-gather.30.cloned.1.call-update) | async-done | bytes 2097168 | tf_op jit(solution)/shard_map/all_gather | solution.py:60
  216.1 16.3 while.74
  232.5 29.6 %all-gather.26.cloned.1.call-done = bf16[2048,512]{1,0:T(8,128)(2,1)} async-done(((bf16[256,512]{1,0:T(8,128)(2,1)}), bf16[2048,512]{1,0:T(8,128)(2,1)}) %all-gather.26.cloned.1.call-update) | async-done | bytes 2097168 | tf_op jit(solution)/shard_map/all_gather | solution.py:61
  266.1 14.3 while.75
  280.4 31.3 %all-gather.34.cloned.1.call-done = bf16[2048,512]{1,0:T(8,128)(2,1)} async-done(((bf16[256,512]{1,0:T(8,128)(2,1)}), bf16[2048,512]{1,0:T(8,128)(2,1)}) %all-gather.34.cloned.1.call-update) | async-done | bytes 2097168 | tf_op jit(solution)/shard_map/all_gather | solution.py:43
  319.8 18.6 all-gather.2
  342.3 30.6 %all_gather.84 = bf16[2048,8]{0,1:T(8,128)(2,1)S(1)} all-gather(bf16[256,8]{0,1:T(8,128)(2,1)S(1)} %copy-done.79), channel_id=1, replica_groups=mesh['cp'=8,'tp'=4] {'cp'}, dimensions={0}, use_global_device_ids=true | all-gather | bytes 36864 | tf_op jit(solution)/shard_map/all_gather | solution.py:53
  375.6 4.2 gather_fusion
  380.4 112.4 %all-gather.36.cloned.1.call-done = bf16[2048,8,256]{2,0,1:T(8,128)(2,1)} async-done(((bf16[256,8,256]{2,0,1:T(8,128)(2,1)}), bf16[2048,8,256]{2,0,1:T(8,128)(2,1)}) %all-gather.36.cloned.1.call-update) | async-done | bytes 8388624 | tf_op jit(solution)/shard_map/all_gather | solution.py:50
  492.8 5.8 fusion.148
  498.6 119.6 %all-gather.40.cloned.1.call-done = bf16[2048,8,256]{2,0,1:T(8,128)(2,1)} async-done(((bf16[256,8,256]{2,0,1:T(8,128)(2,1)}), bf16[2048,8,256]{2,0,1:T(8,128)(2,1)}) %all-gather.40.cloned.1.call-update) | async-done | bytes 8388624 | tf_op jit(solution)/shard_map/all_gather | solution.py:52
  618.2 124.7 %all-gather.38.cloned.1.call-done = bf16[2048,8,256]{2,1,0:T(8,128)(2,1)} async-done(((bf16[256,8,256]{2,1,0:T(8,128)(2,1)}), bf16[2048,8,256]{2,1,0:T(8,128)(2,1)}) %all-gather.38.cloned.1.call-update) | async-done | bytes 8388624 | tf_op jit(solution)/shard_map/all_gather | solution.py:51
  742.9 13.7 fusion.97
  756.6 8.2 gather_fusion.1
  764.8 6.0 reshape.505
  770.9 9.9 multiply_reduce_fusion
  781.1 34.3 %all-reduce.16.cloned.1.call-done = bf16[256,2048]{1,0:T(8,128)(2,1)} async-done(((bf16[256,2048]{1,0:T(8,128)(2,1)}), bf16[256,2048]{1,0:T(8,128)(2,1)}) %all-reduce.16.cloned.1.call-update) | async-done | bytes 1048592 | tf_op jit(solution)/shard_map/psum | solution.py:177
  820.4 20.6 all-gather.3
  841.3 27.2 %all-gather.50.cloned.1.call-done = bf16[2048,512]{1,0:T(8,128)(2,1)} async-done(((bf16[256,512]{1,0:T(8,128)(2,1)}), bf16[2048,512]{1,0:T(8,128)(2,1)}) %all-gather.50.cloned.1.call-update) | async-done | bytes 2097168 | tf_op jit(solution)/shard_map/all_gather | solution.py:40
  871.7 46.6 %all-gather.46.cloned.1.call-done = bf16[2048,512]{1,0:T(8,128)(2,1)} async-done(((bf16[256,512]{1,0:T(8,128)(2,1)}), bf16[2048,512]{1,0:T(8,128)(2,1)}) %all-gather.46.cloned.1.call-update) | async-done | bytes 2097168 | tf_op jit(solution)/shard_map/all_gather | solution.py:41
  927.3 40.7 %all-gather.42.cloned.1.call-done = bf16[2048,512]{1,0:T(8,128)(2,1)} async-done(((bf16[256,512]{1,0:T(8,128)(2,1)}), bf16[2048,512]{1,0:T(8,128)(2,1)}) %all-gather.42.cloned.1.call-update) | async-done | bytes 2097168 | tf_op jit(solution)/shard_map/all_gather | solution.py:42
  972.7 45.4 %all-gather.48.cloned.1.call-done = bf16[2048,512]{1,0:T(8,128)(2,1)} async-done(((bf16[256,512]{1,0:T(8,128)(2,1)}), bf16[2048,512]{1,0:T(8,128)(2,1)}) %all-gather.48.cloned.1.call-update) | async-done | bytes 2097168 | tf_op jit(solution)/shard_map/all_gather | solution.py:60
  1022.4 8.9 while.76
  1031.3 37.1 %all-gather.44.cloned.1.call-done = bf16[2048,512]{1,0:T(8,128)(2,1)} async-done(((bf16[256,512]{1,0:T(8,128)(2,1)}), bf16[2048,512]{1,0:T(8,128)(2,1)}) %all-gather.44.cloned.1.call-update) | async-done | bytes 2097168 | tf_op jit(solution)/shard_map/all_gather | solution.py:61
  1072.9 14.3 while.77
  1087.2 30.7 %all-gather.52.cloned.1.call-done = bf16[2048,512]{1,0:T(8,128)(2,1)} async-done(((bf16[256,512]{1,0:T(8,128)(2,1)}), bf16[2048,512]{1,0:T(8,128)(2,1)}) %all-gather.52.cloned.1.call-update) | async-done | bytes 2097168 | tf_op jit(solution)/shard_map/all_gather | solution.py:43
  1126.9 4.3 gather_fusion.2
  1131.1 18.0 all-gather.4
  1149.2 31.0 %all_gather.96 = bf16[2048,8]{0,1:T(8,128)(2,1)S(1)} all-gather(bf16[256,8]{0,1:T(8,128)(2,1)S(1)} %copy-done.80), channel_id=1, replica_groups=mesh['cp'=8,'tp'=4] {'cp'}, dimensions={0}, use_global_device_ids=true | all-gather | bytes 36864 | tf_op jit(solution)/shard_map/all_gather | solution.py:53
  1184.8 4.3 gather_fusion.3
  1189.5 109.0 %all-gather.58.cloned.1.call-done = bf16[2048,8,256]{2,0,1:T(8,128)(2,1)} async-done(((bf16[256,8,256]{2,0,1:T(8,128)(2,1)}), bf16[2048,8,256]{2,0,1:T(8,128)(2,1)}) %all-gather.58.cloned.1.call-update) | async-done | bytes 8388624 | tf_op jit(solution)/shard_map/all_gather | solution.py:50
  1298.5 6.7 fusion.152
  1305.2 118.0 %all-gather.56.cloned.1.call-done = bf16[2048,8,256]{2,0,1:T(8,128)(2,1)} async-done(((bf16[256,8,256]{2,0,1:T(8,128)(2,1)}), bf16[2048,8,256]{2,0,1:T(8,128)(2,1)}) %all-gather.56.cloned.1.call-update) | async-done | bytes 8388624 | tf_op jit(solution)/shard_map/all_gather | solution.py:51
  1423.2 7.0 multiply_convert_fusion.3
  1430.2 117.9 %all-gather.54.cloned.1.call-done = bf16[2048,8,256]{2,0,1:T(8,128)(2,1)} async-done(((bf16[256,8,256]{2,0,1:T(8,128)(2,1)}), bf16[2048,8,256]{2,0,1:T(8,128)(2,1)}) %all-gather.54.cloned.1.call-update) | async-done | bytes 8388624 | tf_op jit(solution)/shard_map/all_gather | solution.py:52
  1548.1 7.1 fusion.77
  1559.1 5.8 psum.60
  1568.1 6.5 multiply_convert_fusion.4
  1574.6 6.3 fusion.153
  1581.0 8.8 convolution_add_fusion
  1589.8 8.2 gather_fusion.4
  1598.0 5.9 reshape.514
  1603.9 8.3 reduce_sum.291
  1615.7 31.2 %all-reduce.20.cloned.1.call-done = bf16[256,2048]{1,0:T(8,128)(2,1)} async-done(((bf16[256,2048]{1,0:T(8,128)(2,1)}), bf16[256,2048]{1,0:T(8,128)(2,1)}) %all-reduce.20.cloned.1.call-update) | async-done | bytes 1048592 | tf_op jit(solution)/shard_map/psum | solution.py:313
  1653.2 14.2 while.78
  1667.5 42.2 %while.79 = (s32[]{:T(128)}, f32[256,4,128]{0,2,1:T(8,128)}, bf16[4,512,512]{2,1,0:T(8,128)(2,1)}, bf16[4,512,512]{2,1,0:T(8,128)(2,1)}, bf16[4,512,4,128]{3,1,2...) while((s32[]{:T(128)}, f32[256,4,128]{0,2,1:T(8,128)}, ...), condition=%wide.region_47.48_spmd.clone, body=%wide.region_46.47_spmd.clone.sunk | while | flops 675807232 | bytes 35405024 | solution.py:382
  1713.4 65.2 %reduce-scatter.6.cloned.1.call-done = bf16[256,512]{1,0:T(8,128)(2,1)} async-done(((bf16[2048,512]{1,0:T(8,128)(2,1)}), bf16[256,512]{1,0:T(8,128)(2,1)}) %reduce-scatter.6.cloned.1.call-update) | async-done | bytes 262160 | tf_op jit(solution)/shard_map/reduce_scatter | solution.py:385
  1786.7 62.7 %reduce-scatter.8.cloned.1.call-done = bf16[256,512]{1,0:T(8,128)(2,1)} async-done(((bf16[2048,512]{1,0:T(8,128)(2,1)}), bf16[256,512]{1,0:T(8,128)(2,1)}) %reduce-scatter.8.cloned.1.call-update) | async-done | bytes 262160 | tf_op jit(solution)/shard_map/reduce_scatter | solution.py:391
  1855.6 5.8 convolution_convert_fusion
  1861.4 7.7 pad_maximum_fusion.1
  1871.0 6.6 convert_bitcast_fusion.1
  1877.6 5.6 convert_bitcast_fusion.2
  1883.3 5.7 convert_bitcast_fusion
  1889.0 17.0 pad_maximum_fusion
  1909.2 40.0 %all-reduce.6 = (f32[128]{0:T(128)}, f32[128]{0:T(128)}) all-reduce(f32[128]{0:T(128)S(1)} %get-tuple-element.1026, f32[128]{0:T(128)S(1)} %get-tuple-element.882), channel_id=1, replica_groups=mesh['cp'=8,'tp'=4] {'cp','tp'}, use_global_device_ids=true, to_apply=%region_57.58 | all-reduce | flops 256 | bytes 2048 | tf_op jit(solution)/shard_map/psum | solution.py:462
  1951.4 22.8 all-reduce.7
  1978.7 118.4 %reduce-scatter.10.cloned.1.call-done = bf16[256,2048]{0,1:T(8,128)(2,1)} async-done(((bf16[2048,2048]{0,1:T(8,128)(2,1)}), bf16[256,2048]{0,1:T(8,128)(2,1)}) %reduce-scatter.10.cloned.1.call-update) | async-done | bytes 1048592 | tf_op jit(solution)/shard_map/reduce_scatter | solution.py:436
  2102.4 401.5 %reduce-scatter.14.cloned.1.call-done = bf16[256,8,768]{0,2,1:T(8,128)(2,1)} async-done(((bf16[2048,8,768]{0,2,1:T(8,128)(2,1)}), bf16[256,8,768]{0,2,1:T(8,128)(2,1)}) %reduce-scatter.14.cloned.1.call-update) | async-done | bytes 3145744 | tf_op jit(solution)/shard_map/reduce_scatter | solution.py:445
  2504.0 4.6 fusion.141
  (611 shorter events, 256.0 us)
Async XLA Ops:
  7.2 27.2 %copy-start.4 = (bf16[256,2048]{1,0:T(8,128)(2,1)S(1)}, bf16[256,2048]{1,0:T(8,128)(2,1)}, u32[]{:S(2)}) copy-start(bf16[256,2048]{1,0:T(8,128)(2,1)} %param.28) | copy-start | bytes 3145732
  7.2 54.9 %all-gather.32.cloned.1.call-start = ((), (), s32[]{:S(2)}) async-start(), calls=%async_computation.9 | async-start | bytes 2359296 | tf_op jit(solution)/shard_map/all_gather | solution.py:40
  7.9 103.9 %all-gather.28.cloned.1.call-start = ((), (), s32[]{:S(2)}) async-start(), calls=%async_computation.7 | async-start | bytes 2359296 | tf_op jit(solution)/shard_map/all_gather | solution.py:41
  8.7 153.0 %all-gather.24.cloned.1.call-start = ((), (), s32[]{:S(2)}) async-start(), calls=%async_computation.5 | async-start | bytes 2359296 | tf_op jit(solution)/shard_map/all_gather | solution.py:42
  9.4 202.5 %all-gather.30.cloned.1.call-start = ((), (), s32[]{:S(2)}) async-start(), calls=%async_computation.8 | async-start | bytes 2359296 | tf_op jit(solution)/shard_map/all_gather | solution.py:60
  32.5 79.4 %copy-start.90 = (f32[8,1,256]{2,1,0:T(1,128)}, f32[8,1,256]{2,1,0:T(1,128)S(1)}, u32[]{:S(2)}) copy-start(f32[8,1,256]{2,1,0:T(1,128)S(1)} %convert_element_type.268) | copy-start | bytes 24580
  33.1 83.0 %copy-start.73 = (f32[128]{0:T(128)}, f32[128]{0:T(128)S(1)}, u32[]{:S(2)}) copy-start(f32[128]{0:T(128)S(1)} %convert_element_type.216) | copy-start | bytes 1540
  33.8 82.1 %copy-start.81 = (f32[128]{0:T(128)}, f32[128]{0:T(128)S(1)}, u32[]{:S(2)}) copy-start(f32[128]{0:T(128)S(1)} %convert_element_type.213) | copy-start | bytes 1540
  34.1 82.1 %copy-start.30 = (f32[256,128]{0,1:T(8,128)}, f32[256,128]{0,1:T(8,128)S(1)}, u32[]{:S(2)}) copy-start(f32[256,128]{0,1:T(8,128)S(1)} %get-tuple-element.1043) | copy-start | bytes 393220
  34.1 82.0 %copy-start.36 = (f32[256,128]{0,1:T(8,128)}, f32[256,128]{0,1:T(8,128)S(1)}, u32[]{:S(2)}) copy-start(f32[256,128]{0,1:T(8,128)S(1)} %get-tuple-element.1044) | copy-start | bytes 393220
  34.4 84.0 %copy-start.23 = (f32[256,512]{1,0:T(8,128)}, f32[256,512]{1,0:T(8,128)S(1)}, u32[]{:S(2)}) copy-start(f32[256,512]{1,0:T(8,128)S(1)} %copy.417) | copy-start | bytes 1572868
  34.7 29.7 %copy-start.87 = (f32[256]{0:T(256)}, f32[256]{0:T(256)S(1)}, u32[]{:S(2)}) copy-start(f32[256]{0:T(256)S(1)} %fusion.85) | copy-start | bytes 3076
  34.7 77.1 %copy-start.84 = (f32[256]{0:T(256)}, f32[256]{0:T(256)S(1)}, u32[]{:S(2)}) copy-start(f32[256]{0:T(256)S(1)} %fusion.132) | copy-start | bytes 3076
  34.7 83.6 %copy-start.71 = (f32[512]{0:T(512)}, f32[512]{0:T(512)S(1)}, u32[]{:S(2)}) copy-start(f32[512]{0:T(512)S(1)} %broadcast_bitcast_fusion) | copy-start | bytes 6148
  117.3 44.3 %copy-start.85 = (f32[256]{0:T(256)S(1)}, f32[256]{0:T(256)}, u32[]{:S(2)}) copy-start(f32[256]{0:T(256)} %copy-done.84) | copy-start | bytes 3076
  117.3 44.3 %copy-start.91 = (f32[8,1,256]{2,1,0:T(1,128)S(1)}, f32[8,1,256]{2,1,0:T(1,128)}, u32[]{:S(2)}) copy-start(f32[8,1,256]{2,1,0:T(1,128)} %copy-done.90) | copy-start | bytes 24580
  120.4 45.0 %copy-start.48 = (s32[256]{0:T(256)S(1)}, s32[256]{0:T(256)}, u32[]{:S(2)}) copy-start(s32[256]{0:T(256)} %param.29) | copy-start | bytes 3076
  120.4 63.4 %copy-start.47 = (bf16[256,4,128]{0,2,1:T(8,128)(2,1)S(1)}, bf16[256,4,128]{0,2,1:T(8,128)(2,1)}, u32[]{:S(2)}) copy-start(bf16[256,4,128]{0,2,1:T(8,128)(2,1)} %get-tuple-element.1032) | copy-start | bytes 786436
  120.4 141.7 %all-gather.26.cloned.1.call-start = ((), (), s32[]{:S(2)}) async-start(), calls=%async_computation.6 | async-start | bytes 2359296 | tf_op jit(solution)/shard_map/all_gather | solution.py:61
  164.7 147.0 %all-gather.34.cloned.1.call-start = ((), (), s32[]{:S(2)}) async-start(), calls=%async_computation.10 | async-start | bytes 2359296 | tf_op jit(solution)/shard_map/all_gather | solution.py:43
  165.3 207.7 %all-reduce.14.cloned.1.call-start = ((), (), s32[]{:S(2)}) async-start(), calls=%async_computation.11 | async-start | bytes 4194304 | tf_op jit(solution)/shard_map/psum | solution.py:147
  232.5 33.6 %copy-start.52 = (f32[4,256]{1,0:T(4,128)S(1)}, f32[4,256]{1,0:T(4,128)}, u32[]{:S(2)}) copy-start(f32[4,256]{1,0:T(4,128)} %get-tuple-element.297) | copy-start | bytes 12292
  232.5 33.6 %copy-start.49 = (f32[256,4,128]{0,2,1:T(8,128)S(1)}, f32[256,4,128]{0,2,1:T(8,128)}, u32[]{:S(2)}) copy-start(f32[256,4,128]{0,2,1:T(8,128)} %custom-call.2) | copy-start | bytes 1572868
  315.4 177.4 %all-gather.36.cloned.1.call-start = ((), (), s32[]{:S(2)}) async-start(), calls=%async_computation.12 | async-start | bytes 9437184 | tf_op jit(solution)/shard_map/all_gather | solution.py:50
  317.8 24.5 copy-start.79
  317.8 300.4 %all-gather.40.cloned.1.call-start = ((), (), s32[]{:S(2)}) async-start(), calls=%async_computation.14 | async-start | bytes 9437184 | tf_op jit(solution)/shard_map/all_gather | solution.py:52
  319.1 423.8 %all-gather.38.cloned.1.call-start = ((), (), s32[]{:S(2)}) async-start(), calls=%async_computation.13 | async-start | bytes 9437184 | tf_op jit(solution)/shard_map/all_gather | solution.py:51
  319.7 495.7 %all-reduce.16.cloned.1.call-start = ((), (), s32[]{:S(2)}) async-start(), calls=%async_computation.15 | async-start | bytes 2097152 | tf_op jit(solution)/shard_map/psum | solution.py:177
  339.8 35.8 %copy-start.89 = (s32[512,1]{0,1:T(1,128)}, s32[512,1]{0,1:T(1,128)S(1)}, u32[]{:S(2)}) copy-start(s32[512,1]{0,1:T(1,128)S(1)} %compare_select_fusion) | copy-start | bytes 6148
  372.9 383.7 %copy-start.69 = (s32[1024]{0:T(1024)}, s32[1024]{0:T(1024)S(1)}, u32[]{:S(2)}) copy-start(s32[1024]{0:T(1024)S(1)} %pad_clamp_fusion) | copy-start | bytes 12292
  780.8 87.8 %all-gather.50.cloned.1.call-start = ((), (), s32[]{:S(2)}) async-start(), calls=%async_computation.20 | async-start | bytes 2359296 | tf_op jit(solution)/shard_map/all_gather | solution.py:40
  781.1 60.0 %copy-start.11 = (f32[256,2048]{1,0:T(8,128)}, f32[256,2048]{1,0:T(8,128)S(1)}, u32[]{:S(2)}) copy-start(f32[256,2048]{1,0:T(8,128)S(1)} %convert_element_type.209) | copy-start | bytes 6291460
  818.8 99.5 %all-gather.46.cloned.1.call-start = ((), (), s32[]{:S(2)}) async-start(), calls=%async_computation.18 | async-start | bytes 2359296 | tf_op jit(solution)/shard_map/all_gather | solution.py:41
  819.5 148.4 %all-gather.42.cloned.1.call-start = ((), (), s32[]{:S(2)}) async-start(), calls=%async_computation.16 | async-start | bytes 2359296 | tf_op jit(solution)/shard_map/all_gather | solution.py:42
  820.1 198.0 %all-gather.48.cloned.1.call-start = ((), (), s32[]{:S(2)}) async-start(), calls=%async_computation.19 | async-start | bytes 2359296 | tf_op jit(solution)/shard_map/all_gather | solution.py:60
  841.0 29.8 %copy-start.53 = (f32[8,1,256]{2,1,0:T(1,128)}, f32[8,1,256]{2,1,0:T(1,128)S(1)}, u32[]{:S(2)}) copy-start(f32[8,1,256]{2,1,0:T(1,128)S(1)} %convert_element_type.270) | copy-start | bytes 24580
  841.3 29.5 %copy-start.20 = (bf16[256,2048]{1,0:T(8,128)(2,1)}, bf16[256,2048]{1,0:T(8,128)(2,1)S(1)}, u32[]{:S(2)}) copy-start(bf16[256,2048]{1,0:T(8,128)(2,1)S(1)} %multiply_convert_fusion.1) | copy-start | bytes 3145732
  871.3 51.2 %copy-start.14 = (f32[256,4,128]{0,2,1:T(8,128)}, f32[256,4,128]{0,2,1:T(8,128)S(1)}, u32[]{:S(2)}) copy-start(f32[256,4,128]{0,2,1:T(8,128)S(1)} %copy.373) | copy-start | bytes 1572868
  871.7 50.1 %copy-start.65 = (f32[256,4]{0,1:T(4,128)}, f32[256,4]{0,1:T(4,128)S(1)}, u32[]{:S(2)}) copy-start(f32[256,4]{0,1:T(4,128)S(1)} %copy.372) | copy-start | bytes 12292
  923.9 44.0 %copy-start.21 = (bf16[256,2048]{1,0:T(8,128)(2,1)S(1)}, bf16[256,2048]{1,0:T(8,128)(2,1)}, u32[]{:S(2)}) copy-start(bf16[256,2048]{1,0:T(8,128)(2,1)} %copy-done.20) | copy-start | bytes 3145732
  927.0 141.4 %all-gather.44.cloned.1.call-start = ((), (), s32[]{:S(2)}) async-start(), calls=%async_computation.17 | async-start | bytes 2359296 | tf_op jit(solution)/shard_map/all_gather | solution.py:61
  971.0 147.0 %all-gather.52.cloned.1.call-start = ((), (), s32[]{:S(2)}) async-start(), calls=%async_computation.21 | async-start | bytes 2359296 | tf_op jit(solution)/shard_map/all_gather | solution.py:43
  971.6 208.6 %all-reduce.18.cloned.1.call-start = ((), (), s32[]{:S(2)}) async-start(), calls=%async_computation.22 | async-start | bytes 4194304 | tf_op jit(solution)/shard_map/psum | solution.py:147
  1087.2 34.4 %copy-start.32 = (bf16[256,4,128]{0,2,1:T(8,128)(2,1)}, bf16[256,4,128]{0,2,1:T(8,128)(2,1)S(1)}, u32[]{:S(2)}) copy-start(bf16[256,4,128]{0,2,1:T(8,128)(2,1)S(1)} %convert_element_type.232) | copy-start | bytes 786436
  1121.7 176.8 %all-gather.58.cloned.1.call-start = ((), (), s32[]{:S(2)}) async-start(), calls=%async_computation.25 | async-start | bytes 9437184 | tf_op jit(solution)/shard_map/all_gather | solution.py:50
  1124.1 299.1 %all-gather.56.cloned.1.call-start = ((), (), s32[]{:S(2)}) async-start(), calls=%async_computation.24 | async-start | bytes 9437184 | tf_op jit(solution)/shard_map/all_gather | solution.py:51
  1125.3 422.7 %all-gather.54.cloned.1.call-start = ((), (), s32[]{:S(2)}) async-start(), calls=%async_computation.23 | async-start | bytes 9437184 | tf_op jit(solution)/shard_map/all_gather | solution.py:52
  1126.6 22.5 copy-start.80
  1126.7 520.2 %all-reduce.20.cloned.1.call-start = ((), (), s32[]{:S(2)}) async-start(), calls=%async_computation.26 | async-start | bytes 2097152 | tf_op jit(solution)/shard_map/psum | solution.py:313
  1430.2 125.0 %copy-start.42 = (bf16[8,96,256]{2,1,0:T(8,128)(2,1)}, bf16[8,96,256]{2,1,0:T(8,128)(2,1)S(1)}, u32[]{:S(2)}) copy-start(bf16[8,96,256]{2,1,0:T(8,128)(2,1)S(1)} %get-tuple-element.1040) | copy-start | bytes 1179652
  1612.2 166.4 %reduce-scatter.6.cloned.1.call-start = ((), (), s32[]{:S(2)}) async-start(), calls=%async_computation.27 | async-start | bytes 2359296 | tf_op jit(solution)/shard_map/reduce_scatter | solution.py:385
  1615.6 34.7 %copy-start.63 = (bf16[256,8]{0,1:T(8,128)(2,1)}, bf16[256,8]{0,1:T(8,128)(2,1)S(1)}, u32[]{:S(2)}) copy-start(bf16[256,8]{0,1:T(8,128)(2,1)S(1)} %multiply_convert_fusion.5) | copy-start | bytes 12292
  1709.8 139.6 %reduce-scatter.8.cloned.1.call-start = ((), (), s32[]{:S(2)}) async-start(), calls=%async_computation.28 | async-start | bytes 2359296 | tf_op jit(solution)/shard_map/reduce_scatter | solution.py:391
  1710.4 197.6 %reduce-scatter.12.cloned.1.call-start = ((), (), s32[]{:S(2)}) async-start(), calls=%async_computation.31 | async-start | bytes 36864 | tf_op jit(solution)/shard_map/reduce_scatter | solution.py:452
  1711.3 68.4 %copy-start.38 = (f32[256,128]{0,1:T(8,128)S(1)}, f32[256,128]{0,1:T(8,128)}, u32[]{:S(2)}) copy-start(f32[256,128]{0,1:T(8,128)} %copy-done.36) | copy-start | bytes 393220
  1711.3 237.8 %all-reduce.22.cloned.1.call-start = ((), (), s32[]{:S(2)}) async-start(), calls=%async_computation.29 | async-start | bytes 2097152 | tf_op jit(solution)/shard_map/psum | solution.py:423
  1855.6 241.5 %reduce-scatter.10.cloned.1.call-start = ((), (), s32[]{:S(2)}) async-start(), calls=%async_computation.30 | async-start | bytes 9437184 | tf_op jit(solution)/shard_map/reduce_scatter | solution.py:436
  1869.1 634.8 %reduce-scatter.14.cloned.1.call-start = ((), (), s32[]{:S(2)}) async-start(), calls=%async_computation.32 | async-start | bytes 28311552 | tf_op jit(solution)/shard_map/reduce_scatter | solution.py:445
  1906.0 43.1 %copy-start.5 = (bf16[256,2048]{1,0:T(8,128)(2,1)S(1)}, bf16[256,2048]{1,0:T(8,128)(2,1)}, u32[]{:S(2)}) copy-start(bf16[256,2048]{1,0:T(8,128)(2,1)} %param.28) | copy-start | bytes 3145732
  1906.0 43.1 %copy-start.54 = (f32[8,1,256]{2,1,0:T(1,128)S(1)}, f32[8,1,256]{2,1,0:T(1,128)}, u32[]{:S(2)}) copy-start(f32[8,1,256]{2,1,0:T(1,128)} %copy-done.53) | copy-start | bytes 24580
  1906.0 43.1 %copy-start.86 = (f32[256]{0:T(256)S(1)}, f32[256]{0:T(256)}, u32[]{:S(2)}) copy-start(f32[256]{0:T(256)} %copy-done.84) | copy-start | bytes 3076
  1906.1 45.4 %copy-start.78 = (bf16[2048]{0:T(1024)(128)(2,1)S(1)}, bf16[2048]{0:T(1024)(128)(2,1)}, u32[]{:S(2)}) copy-start(bf16[2048]{0:T(1024)(128)(2,1)} %get-tuple-element.878) | copy-start | bytes 12292
  1906.1 69.4 %copy-start.88 = (f32[256]{0:T(256)S(1)}, f32[256]{0:T(256)}, u32[]{:S(2)}) copy-start(f32[256]{0:T(256)} %copy-done.87) | copy-start | bytes 3076
  1906.1 69.4 %copy-start.8 = (f32[256,2048]{1,0:T(8,128)S(1)}, f32[256,2048]{1,0:T(8,128)}, u32[]{:S(2)}) copy-start(f32[256,2048]{1,0:T(8,128)} %copy-done.6) | copy-start | bytes 6291460
  (72 other events, 190.4 us)
Sparse Core Ops, SparseCore 0:
  10.1 51.9 all-gather.31
  64.2 47.6 all-gather.27
  114.0 47.6 all-gather.23
  164.2 47.6 all-gather.29
  214.4 47.6 all-gather.25
  264.1 47.5 all-gather.33
  315.5 49.9 all-reduce.13
  368.2 124.5 all-gather.35
  495.6 122.6 all-gather.39
  620.2 122.6 all-gather.37
  780.9 34.4 all-reduce.15
  818.9 49.5 all-gather.49
  870.7 47.6 all-gather.45
  920.3 47.6 all-gather.41
  970.5 47.6 all-gather.47
  1020.7 47.6 all-gather.43
  1070.3 47.6 all-gather.51
  1121.8 49.9 all-reduce.17
  1173.9 124.5 all-gather.57
  1300.5 122.6 all-gather.55
  1425.4 122.6 all-gather.53
  1612.3 34.5 all-reduce.19
  1709.9 68.7 reduce-scatter.5
  1782.0 67.3 reduce-scatter.7
  1852.5 53.7 reduce-scatter.11
  1909.1 35.4 all-reduce.21
  1948.0 149.0 reduce-scatter.9
  2101.0 402.9 reduce-scatter.13
where the time goes:
time: 2540 us; the launch traced here: 2520 us
  waiting for transfers between devices  1850 us (73%)
  blocking collectives  228 us (9%)
  matrix products  194 us (8%)
  local copies, waits for them, and re-layouts  143 us (6%)
  other arithmetic  85.8 us (3%)
    reduce_scatter x1, waiting for transfers between devices, on_device(): lax.psum_scatter(jnp.concatenate([gate_term, up_term, down_term], axis=2)...  402 us
    all_gather x2, waiting for transfers between devices, gather_experts(): lax.all_gather(w_up, 'cp', axis=0, tiled=True)  243 us
    all_gather x2, waiting for transfers between devices, gather_experts(): lax.all_gather(w_down, 'cp', axis=0, tiled=True)  238 us
    all_gather x2, waiting for transfers between devices, gather_experts(): lax.all_gather(w_gate, 'cp', axis=0, tiled=True)  221 us
    reduce_scatter x1, waiting for transfers between devices, on_device(): lax.psum_scatter(jnp.concatenate([front_part, back_part], axis=1).astype(...  118 us
    all_gather x2, waiting for transfers between devices, gather_attention(): lax.all_gather(w_key, 'cp', axis=0, tiled=True)  93.2 us
    all_gather x2, waiting for transfers between devices, gather_attention(): lax.all_gather(w_value, 'cp', axis=0, tiled=True)  81.9 us
    all_gather x2, waiting for transfers between devices, gather_keys(): lax.all_gather(k_flat, 'cp', axis=0, tiled=True)  73.4 us
  transfers between devices with their start and end apart: 28, of which 24 were waited for; matrix products, arithmetic and copies ran while one was open for 9% of the time, Pallas kernels for 0%

commit v1 on v0

v1 whole, which is shorter than its diff:
```python
import functools
import itertools

import jax
import jax.numpy as jnp
from jax import lax
from jax.experimental import pallas as pl
from jax.experimental.pallas import tpu as pltpu
from jax.sharding import Mesh
from jax.sharding import PartitionSpec as P

eps = 1e-05
theta = 50000.0
negative = -1e30
AXES = ("b", "a", "y", "c")
TP = ("y", "c")
MESH = pl.DeviceIdType.MESH
bf16 = jnp.bfloat16
f32 = jnp.float32


def exchange(sizes, cid, items):
    counts = []
    outs = []
    for kind, axes, array, space in items:
        count = 1
        for axis in axes:
            count *= sizes[axis]
        counts.append(count)
        block = array.shape if kind == "all" else array.shape[1:]
        outs.append(jax.ShapeDtypeStruct((count,) + tuple(block), array.dtype))

    plans = []
    peers = []
    for (kind, axes, array, space), count in zip(items, counts):
        plan = []
        for offs in itertools.product(*[range(sizes[axis]) for axis in axes]):
            if not any(offs):
                continue
            full = tuple(offs[axes.index(axis)] if axis in axes else 0 for axis in AXES)
            plan.append(full)
            if full not in peers:
                peers.append(full)
        plans.append(plan)
    total = sum(len(plan) for plan in plans)
    number = len(items)

    def kernel(*refs):
        ins, dst = refs[:number], refs[number : 2 * number]
        send, recv, local = refs[2 * number :]
        me = {axis: lax.axis_index(axis) for axis in AXES}

        def there(full):
            return {
                axis: lax.rem(me[axis] + off, sizes[axis]) for axis, off in zip(AXES, full) if off
            }

        def rank(axes, place):
            index = 0
            for axis in axes:
                index = index * sizes[axis] + place.get(axis, me[axis])
            return index

        barrier = pltpu.get_barrier_semaphore()
        for full in peers:
            pl.semaphore_signal(barrier, inc=1, device_id=there(full), device_id_type=MESH)
        pl.semaphore_wait(barrier, len(peers))
        copies = []
        slot = 0
        for i, (kind, axes, array, space) in enumerate(items):
            mine = rank(axes, {})
            for full in plans[i]:
                place = there(full)
                source = ins[i] if kind == "all" else ins[i].at[rank(axes, place)]
                copy = pltpu.make_async_remote_copy(
                    src_ref=source,
                    dst_ref=dst[i].at[mine],
                    send_sem=send.at[slot],
                    recv_sem=recv.at[slot],
                    device_id=place,
                    device_id_type=MESH,
                )
                copy.start()
                copies.append(copy)
                slot += 1
        for i, (kind, axes, array, space) in enumerate(items):
            mine = rank(axes, {})
            source = ins[i] if kind == "all" else ins[i].at[mine]
            copy = pltpu.make_async_copy(source, dst[i].at[mine], local.at[i])
            copy.start()
            copies.append(copy)
        for copy in copies:
            copy.wait()

    spaces = [
        pl.BlockSpec(memory_space=pltpu.VMEM if item[3] == "v" else pl.ANY) for item in items
    ]
    return pl.pallas_call(
        kernel,
        out_shape=outs,
        in_specs=spaces,
        out_specs=spaces,
        scratch_shapes=[
            pltpu.SemaphoreType.DMA((total,)),
            pltpu.SemaphoreType.DMA((total,)),
            pltpu.SemaphoreType.DMA((number,)),
        ],
        compiler_params=pltpu.CompilerParams(collective_id=cid, has_side_effects=True),
    )(*[item[2] for item in items])


def pack(vector):
    flat = vector.reshape(-1)
    flat = flat if flat.dtype == jnp.int32 else flat.astype(f32)
    extra = -flat.shape[0] % 1024
    return jnp.pad(flat, (0, extra)).reshape(-1, 128)


def unpack(packed, lead, shape):
    count = 1
    for size in shape:
        count *= size
    return packed.reshape(lead, -1)[:, :count].reshape((lead,) + tuple(shape))


def rms_norm(values, gain_vec):
    factor = lax.rsqrt(jnp.mean(values * values, axis=-1, keepdims=True) + eps)
    return values * factor * gain_vec


def rotary_tables(positions, head_dim):
    half_dim = head_dim // 2
    inverse_freq = theta ** (-2.0 * jnp.arange(half_dim, dtype=f32) / head_dim)
    angles = positions[:, None] * inverse_freq[None, :]
    cos_tab = jnp.concatenate([jnp.cos(angles), jnp.cos(angles)], axis=-1)
    sin_tab = jnp.concatenate([jnp.sin(angles), jnp.sin(angles)], axis=-1)
    return (cos_tab, sin_tab)


def rotate_half(tensor):
    half_dim = tensor.shape[-1] // 2
    return jnp.concatenate([-tensor[..., half_dim:], tensor[..., :half_dim]], axis=-1)


def qk_prepare(raw, gain_vec, cos_tab, sin_tab):
    normed = rms_norm(raw, gain_vec)
    return normed * cos_tab + rotate_half(normed) * sin_tab


NT = (((1,), (1,)), ((), ()))
TN = (((0,), (0,)), ((), ()))


def dot(left, right, dims=(((1,), (0,)), ((), ()))):
    return lax.dot_general(left, right, dims, preferred_element_type=f32)


def attend_kernel(scale, q_ref, kv_ref, dq_ref, dk_ref, out_ref, norm_ref):
    head = q_ref.shape[1]
    keys, values = kv_ref[:, :head], kv_ref[:, head:]
    scores = dot(q_ref[...], keys, NT) * scale
    keep = dq_ref[...] == dk_ref[...]
    scores = jnp.where(keep, scores, negative)
    top = jnp.max(scores, axis=1, keepdims=True)
    terms = jnp.exp(scores - top)
    total = jnp.sum(terms, axis=1, keepdims=True)
    probs = (terms * (1.0 / total)).astype(bf16)
    out_ref[...] = dot(probs, values).astype(bf16)
    norm_ref[...] = top + jnp.log(total)


def attend(q_rot, kv, docs_q, docs_k, scale):
    rows, head = q_rot.shape
    keys = kv.shape[0]
    tile = 256
    return pl.pallas_call(
        functools.partial(attend_kernel, scale),
        grid=(rows // tile,),
        out_shape=[
            jax.ShapeDtypeStruct((rows, head), bf16),
            jax.ShapeDtypeStruct((rows, 1), f32),
        ],
        in_specs=[
            pl.BlockSpec((tile, head), lambda i: (i, 0)),
            pl.BlockSpec((keys, 2 * head), lambda i: (0, 0)),
            pl.BlockSpec((tile, 1), lambda i: (i, 0)),
            pl.BlockSpec((1, keys), lambda i: (0, 0)),
        ],
        out_specs=[
            pl.BlockSpec((tile, head), lambda i: (i, 0)),
            pl.BlockSpec((tile, 1), lambda i: (i, 0)),
        ],
    )(q_rot, kv, docs_q[:, None], docs_k[None, :])


def attend_back_kernel(
    scale, q_ref, kv_ref, dq_ref, dk_ref, norm_ref, cot_ref, qgrad_ref, kvgrad_ref
):
    head = q_ref.shape[1]
    queries, cot = q_ref[...], cot_ref[...]
    keys, values = kv_ref[:, :head], kv_ref[:, head:]
    scores = dot(queries, keys, NT) * scale
    keep = dq_ref[...] == dk_ref[...]
    probs = jnp.where(keep, jnp.exp(scores - norm_ref[...]), 0.0)
    d_soft = dot(cot, values, NT)
    delta = jnp.sum(probs * d_soft, axis=1, keepdims=True)
    d_scores = (probs * (d_soft - delta)).astype(bf16)
    qgrad_ref[...] = dot(d_scores, keys) * scale

    @pl.when(pl.program_id(0) == 0)
    def _():
        kvgrad_ref[...] = jnp.zeros_like(kvgrad_ref)

    kvgrad_ref[:, :head] += dot(d_scores, queries, TN) * scale
    kvgrad_ref[:, head:] += dot(probs.astype(bf16), cot, TN)


def attend_back(q_rot, kv, docs_q, docs_k, norm, cot, scale):
    rows, head = q_rot.shape
    keys = kv.shape[0]
    tile = 256 if keys <= 4096 else 128
    return pl.pallas_call(
        functools.partial(attend_back_kernel, scale),
        grid=(rows // tile,),
        out_shape=[
            jax.ShapeDtypeStruct((rows, head), f32),
            jax.ShapeDtypeStruct((keys, 2 * head), f32),
        ],
        in_specs=[
            pl.BlockSpec((tile, head), lambda i: (i, 0)),
            pl.BlockSpec((keys, 2 * head), lambda i: (0, 0)),
            pl.BlockSpec((tile, 1), lambda i: (i, 0)),
            pl.BlockSpec((1, keys), lambda i: (0, 0)),
            pl.BlockSpec((tile, 1), lambda i: (i, 0)),
            pl.BlockSpec((tile, head), lambda i: (i, 0)),
        ],
        out_specs=[
            pl.BlockSpec((tile, head), lambda i: (i, 0)),
            pl.BlockSpec((keys, 2 * head), lambda i: (0, 0)),
        ],
    )(q_rot, kv, docs_q[:, None], docs_k[None, :], norm, cot)


def on_device(
    sizes,
    tokens_in,
    doc_ids,
    expert_ids,
    attn_gain,
    q_gain,
    k_gain,
    w_query,
    w_key,
    w_value,
    w_output,
    ffn_gain,
    w_router,
    w_gate,
    w_up,
    w_down,
    cotangent,
):
    nb, na = sizes["b"], sizes["a"]
    nt = sizes["y"] * sizes["c"]
    tok, model = tokens_in.shape
    col = nb * tok
    part = model // nb
    sub = part // na
    head = q_gain.shape[0]
    width = w_query.shape[1]
    heads = width // head
    experts, ff = w_gate.shape[1], w_gate.shape[2]
    top = expert_ids.shape[1]
    quarter = tok // nt
    scale = head**-0.5
    comm = functools.partial(exchange, sizes)
    a_me = lax.axis_index("a")
    t_me = lax.axis_index("y") * sizes["c"] + lax.axis_index("c")

    def blocks(array):
        return array.reshape(tok, nb, part).transpose(1, 0, 2)

    def share(array):
        rest = array.shape[1]
        array = array.reshape(nb, nt, quarter, rest).transpose(1, 0, 2, 3)
        return array.reshape(nt, nb * quarter, rest)

    def unshare(array):
        rest = array.shape[-1]
        array = array.reshape(nt, nb, quarter, rest).transpose(1, 0, 2, 3)
        return array.reshape(col, rest)

    def own(array):
        rest = array.shape[1]
        array = array.reshape(nb, nt, quarter, rest)
        return lax.dynamic_index_in_dim(array, t_me, 1, keepdims=False).reshape(nb * quarter, rest)

    tokens = tokens_in.astype(f32)
    r_own = lax.rsqrt(jnp.mean(tokens * tokens, axis=-1) + eps)
    got = comm(
        1,
        [
            ("each", ("b",), blocks(tokens_in), "v"),
            ("all", ("a",), w_query, "v"),
            ("all", ("a",), w_key, "v"),
            ("all", ("a",), w_value, "v"),
            ("all", ("b",), pack(r_own), "v"),
            ("all", ("a",), pack(attn_gain), "v"),
            ("all", ("b",), pack(expert_ids), "v"),
            ("all", ("b", "a"), pack(doc_ids), "v"),
        ],
    )
    xc = got[0].reshape(col, part)
    wq, wk, wv = [w.reshape(part, heads, head) for w in got[1:4]]
    r_in = unpack(got[4], nb, (tok,)).reshape(col, 1)
    gain_in = unpack(got[5], na, (sub,)).reshape(1, part)
    chosen = unpack(got[6], nb, (tok, top)).reshape(col, top)
    docs = unpack(got[7], nb * na, (tok,)).reshape(nb, na, tok)
    docs_k = docs.transpose(1, 0, 2).reshape(-1)
    docs_q = lax.dynamic_index_in_dim(docs, a_me, 1, keepdims=False).reshape(col)

    normed_in = (xc.astype(f32) * r_in * gain_in).astype(bf16)
    w_qkv = jnp.stack([wq, wk, wv], axis=2)
    flat_qkv = w_qkv.reshape(part, heads * 3 * head)
    qkv_part = dot(normed_in, flat_qkv).astype(bf16)
    qkv_part = qkv_part.reshape(col, heads, 3 * head).transpose(1, 0, 2)

    got = comm(
        2,
        [
            ("each", ("b",), qkv_part, "v"),
            ("all", ("a",), w_output, "h"),
            ("all", ("a",), w_down, "h"),
            ("all", ("a",), w_gate, "h"),
            ("all", ("a",), w_up, "h"),
            ("all", ("a",), pack(ffn_gain), "v"),
            ("all", ("a",), pack(w_router), "v"),
        ],
    )
    raw = jnp.sum(got[0].astype(f32), axis=0)
    wo = got[1].reshape(part, width)
    wd, wg, wu = [w.reshape(part, experts * ff) for w in got[2:5]]
    gain_mid = unpack(got[5], na, (sub,)).reshape(1, part)
    router = unpack(got[6], na, (sub, experts)).reshape(part, experts).astype(bf16)

    q_raw, k_raw, v_raw = raw[:, :head], raw[:, head : 2 * head], raw[:, 2 * head :]
    index = jnp.arange(col, dtype=jnp.int32)
    positions = ((index // tok * na + a_me) * tok + index % tok).astype(f32)
    cos_tab, sin_tab = rotary_tables(positions, head)
    q_rot, q_back = jax.vjp(
        lambda u, g: qk_prepare(u, g, cos_tab, sin_tab), q_raw, q_gain.astype(f32)
    )
    k_rot, k_back = jax.vjp(
        lambda u, g: qk_prepare(u, g, cos_tab, sin_tab), k_raw, k_gain.astype(f32)
    )
    q_rot = q_rot.astype(bf16)
    kv_own = jnp.concatenate([k_rot.astype(bf16), v_raw.astype(bf16)], axis=1)

    got = comm(
        3,
        [("all", ("a",), kv_own, "v"), ("each", ("b",), blocks(cotangent), "v")],
    )
    kv = got[0].reshape(na * col, 2 * head)
    cotc = got[1].reshape(col, part)
    heads_own, norm = attend(q_rot, kv, docs_q, docs_k, scale)

    expert_range = jnp.arange(experts, dtype=jnp.int32)

    def select(array):
        array = array.reshape(col, experts, -1)
        picked = [
            jnp.sum(
                jnp.where((chosen[:, k : k + 1] == expert_range)[:, :, None], array, 0), axis=1
            )
            for k in range(top)
        ]
        return jnp.stack(picked, axis=1)

    def spread(array):
        total = 0
        for k in range(top):
            mask = (chosen[:, k : k + 1] == expert_range)[:, :, None]
            total = total + jnp.where(mask, array[:, k, None, :], jnp.zeros((), array.dtype))
        return total.reshape(col, -1)

    cot_down = select(dot(cotc, wd).astype(bf16)).reshape(nb, tok, top * ff)
    got = comm(
        4,
        [("all", ("b",), heads_own, "v"), ("each", ("b",), cot_down, "v")],
    )
    heads_out = got[0].transpose(1, 0, 2).reshape(col, width)
    down_cot = jnp.sum(got[1].astype(f32), axis=0).reshape(tok, top, ff)
    attn_part = dot(heads_out, wo, NT).astype(bf16)
    got = comm(5, [("each", TP, share(attn_part), "v")])
    hidden = own(xc).astype(f32) + jnp.sum(got[0].astype(f32), axis=0)
    scaled = (hidden * gain_mid).astype(bf16)
    squares = jnp.sum(hidden * hidden, axis=1)
    logit_part = dot(scaled, router)
    small = jnp.concatenate(
        [logit_part.T, squares[None], jnp.zeros((15 - experts, squares.shape[0]), f32)], axis=0
    )
    got = comm(6, [("all", TP, scaled, "v"), ("all", TP, small, "v")])
    scaled_all = unshare(got[0])
    small_all = (
        got[1].reshape(nt, 16, nb, quarter).transpose(2, 1, 0, 3).reshape(nb, 16, nt * quarter)
    )
    gate_part = select(dot(scaled_all, wg).astype(bf16))
    up_part = select(dot(scaled_all, wu).astype(bf16))
    pre_part = jnp.concatenate([gate_part, up_part], axis=2).reshape(nb, tok, top * 2 * ff)
    got = comm(7, [("each", ("b",), pre_part, "v"), ("each", ("b",), small_all, "v")])
    pre = jnp.sum(got[0].astype(f32), axis=0).reshape(tok, top, 2 * ff)
    small = jnp.sum(got[1], axis=0)
    r_mid = lax.rsqrt(small[experts] / model + eps)
    logits = small[:experts].T * r_mid[:, None]
    router_probs = jax.nn.softmax(logits, axis=-1)
    picked = (expert_ids[:, :, None] == expert_range).astype(f32)
    combine = jnp.sum(router_probs[:, None, :] * picked, axis=-1)
    pre = pre * r_mid[:, None, None]
    gate_pre, up_pre = pre[:, :, :ff], pre[:, :, ff:]
    sig = 1.0 / (1.0 + jnp.exp(-gate_pre))
    silu = gate_pre * sig
    act = silu * up_pre
    d_act = combine[:, :, None] * down_cot
    d_gate = d_act * up_pre * (sig * (1.0 + gate_pre * (1.0 - sig)))
    d_up = d_act * silu
    pay = jnp.stack(
        [
            (combine[:, :, None] * act).astype(bf16),
            (d_gate * r_mid[:, None, None]).astype(bf16),
            (d_up * r_mid[:, None, None]).astype(bf16),
        ],
        axis=1,
    ).reshape(tok, 3 * top * ff)
    d_combine_part = jnp.sum(act * down_cot, axis=2)
    inner_part = jnp.sum(d_gate * gate_pre + d_up * up_pre, axis=(1, 2))
    small = jnp.concatenate(
        [d_combine_part.T, inner_part[None], jnp.zeros((7 - top, tok), f32)], axis=0
    )
    got = comm(8, [("all", ("b",), pay, "v"), ("all", TP, small, "v")])
    pay_all = got[0].reshape(col, 3, top, ff)
    small = jnp.sum(got[1], axis=0)
    d_combine, inner = small[:top].T, small[top]
    d_probs = jnp.sum(d_combine[:, :, None] * picked, axis=1)
    d_logits = router_probs * (d_probs - jnp.sum(router_probs * d_probs, axis=-1, keepdims=True))
    inner = inner + jnp.sum(d_logits * logits, axis=1)
    back = r_mid * r_mid * inner / model
    small = jnp.concatenate(
        [(d_logits * r_mid[:, None]).T, back[None], jnp.zeros((15 - experts, tok), f32)], axis=0
    )
    wide_act, wide_gate, wide_up = [spread(pay_all[:, i]) for i in range(3)]
    mid_part = (dot(wide_gate, wg, NT) + dot(wide_up, wu, NT)).astype(bf16)
    mix_part = dot(wide_act, wd, NT).astype(bf16)
    got = comm(
        9,
        [
            ("each", TP, share(mid_part), "v"),
            ("each", TP, share(mix_part), "v"),
            ("all", ("b",), small, "v"),
        ],
    )
    small = got[2]
    small_all = small.transpose(0, 2, 1).reshape(col, 16)
    small_own = own(small_all)
    dl_all = small_all[:, :experts].astype(bf16)
    mid = jnp.sum(got[0].astype(f32), axis=0) + dot(
        small_own[:, :experts].astype(bf16), router, NT
    )
    d_hidden = own(cotc).astype(f32) + gain_mid * mid - hidden * small_own[:, experts : experts + 1]
    ffn_gain_part = jnp.sum(mid * hidden, axis=0)
    d_attn = d_hidden.astype(bf16)
    out_own = (hidden + jnp.sum(got[1].astype(f32), axis=0)).astype(bf16)
    router_part = dot(scaled_all, dl_all, TN)
    got = comm(
        10,
        [("all", TP, d_attn, "v"), ("each", ("b",), out_own.reshape(nb, quarter, part), "v")],
    )
    d_attn_all = unshare(got[0])
    out_rows = got[1].transpose(1, 0, 2).reshape(quarter, model)
    d_heads_part = dot(d_attn_all, wo).astype(bf16).reshape(col, heads, head).transpose(1, 0, 2)
    output_part = dot(d_attn_all, heads_out, TN).astype(bf16)
    got = comm(
        11,
        [
            ("each", ("b",), d_heads_part, "v"),
            ("all", TP, out_rows, "v"),
            ("all", ("a",) + TP, pack(ffn_gain_part), "v"),
        ],
    )
    d_heads = jnp.sum(got[0].astype(f32), axis=0).astype(bf16)
    block_out = got[1].reshape(tok, model)
    ffn_gain_sum = jnp.sum(unpack(got[2], na * nt, (part,)), axis=0).reshape(na, sub)
    grad_ffn_gain = lax.dynamic_index_in_dim(ffn_gain_sum, a_me, 0, keepdims=False)

    d_q_rot, d_kv = attend_back(q_rot, kv, docs_q, docs_k, norm, d_heads, scale)
    gate_grad = dot(scaled_all, wide_gate, TN).astype(bf16).reshape(na, sub, experts * ff)
    up_grad = dot(scaled_all, wide_up, TN).astype(bf16).reshape(na, sub, experts * ff)
    down_grad = dot(cotc, wide_act, TN).astype(bf16).reshape(na, sub, experts * ff)
    got = comm(12, [("each", ("a",), d_kv.astype(bf16).reshape(na, col, 2 * head), "v")])
    d_kv = jnp.sum(got[0].astype(f32), axis=0)
    d_q_raw, q_gain_part = q_back(d_q_rot)
    d_k_raw, k_gain_part = k_back(d_kv[:, :head])
    d_v_raw = d_kv[:, head:]
    inner_part = jnp.sum(d_q_raw * q_raw + d_k_raw * k_raw + d_v_raw * v_raw, axis=1)
    d_qkv = jnp.concatenate([d_q_raw, d_k_raw, d_v_raw], axis=1).astype(bf16)
    got = comm(
        13,
        [
            ("all", ("b",), d_qkv, "v"),
            ("each", ("a",), gate_grad, "h"),
            ("each", ("a",), up_grad, "h"),
            ("each", ("a",), down_grad, "h"),
            ("all", ("b",), pack(inner_part), "v"),
            ("all", ("b",), pack(jnp.concatenate([q_gain_part, k_gain_part])), "v"),
        ],
    )
    d_qkv_all = got[0].transpose(1, 0, 2).reshape(col, heads * 3 * head)
    grad_gate, grad_up, grad_down = [
        jnp.sum(g.astype(f32), axis=0).reshape(sub, experts, ff) for g in got[1:4]
    ]
    inner_part = jnp.sum(unpack(got[4], nb, (col,)), axis=0)
    head_gain_part = jnp.sum(got[5], axis=0)
    in_part = dot(d_qkv_all, flat_qkv, NT).astype(bf16)
    qkv_grad = dot(normed_in, d_qkv_all, TN).astype(bf16).reshape(na, sub, heads * 3 * head)
    inner_share = share(inner_part[:, None]).reshape(nt, -1)
    inner_share = jnp.pad(inner_share, ((0, 0), (0, -inner_share.shape[1] % 1024)))
    got = comm(
        14,
        [
            ("each", TP, share(in_part), "v"),
            ("each", TP, inner_share.reshape(nt, -1, 128), "v"),
            ("each", ("a",), qkv_grad, "v"),
            ("each", ("a",), output_part.reshape(na, sub, width), "v"),
            ("each", ("a",), jax.vmap(pack)(router_part.reshape(na, sub * experts)), "v"),
            ("all", ("a",) + TP, head_gain_part, "v"),
        ],
    )
    d_in = jnp.sum(got[0].astype(f32), axis=0)
    inner = jnp.sum(got[1].reshape(nt, -1), axis=0)[: nb * quarter, None]
    qkv_grad = jnp.sum(got[2].astype(f32), axis=0).reshape(sub, heads, 3, head)
    grad_query, grad_key, grad_value = [qkv_grad[:, :, i].reshape(sub, width) for i in range(3)]
    grad_output = jnp.sum(got[3].astype(f32), axis=0)
    grad_router = jnp.sum(unpack(got[4], na, (sub, experts)), axis=0)
    head_gains = jnp.sum(unpack(got[5], na * nt, (2, head)), axis=0)
    x_own = own(xc).astype(f32)
    r_q = own(r_in)
    grad_in = d_hidden + r_q * gain_in * d_in - x_own * (r_q * r_q * inner / model)
    attn_gain_part = jnp.sum(d_in * x_own * r_q, axis=0)
    got = comm(
        15,
        [
            ("each", ("b",), grad_in.astype(bf16).reshape(nb, quarter, part), "v"),
            ("all", ("a",) + TP, pack(attn_gain_part), "v"),
        ],
    )
    in_rows = got[0].transpose(1, 0, 2).reshape(quarter, model)
    attn_gain_sum = jnp.sum(unpack(got[1], na * nt, (part,)), axis=0).reshape(na, sub)
    grad_attn_gain = lax.dynamic_index_in_dim(attn_gain_sum, a_me, 0, keepdims=False)
    got = comm(16, [("all", TP, in_rows, "v")])
    grad_in = got[0].reshape(tok, model).astype(f32)
    return (
        block_out,
        grad_in,
        grad_attn_gain,
        head_gains[0],
        head_gains[1],
        grad_query,
        grad_key,
        grad_value,
        grad_output,
        grad_ffn_gain,
        grad_router,
        grad_gate,
        grad_up,
        grad_down,
    )


def solution(mesh):
    cp, tp = mesh.shape["cp"], mesh.shape["tp"]
    sizes = {"b": 4, "a": cp // 4, "y": 2, "c": tp // 2}
    split = Mesh(mesh.devices.reshape([sizes[axis] for axis in AXES]), AXES)
    cp, tp = ("b", "a"), ("y", "c")
    return jax.shard_map(
        functools.partial(on_device, sizes),
        mesh=split,
        in_specs=(
            P(cp, None),
            P(cp),
            P(cp, None),
            P(cp),
            P(),
            P(),
            P(cp, tp),
            P(cp, tp),
            P(cp, tp),
            P(cp, tp),
            P(cp),
            P(cp, None),
            P(cp, None, tp),
            P(cp, None, tp),
            P(cp, None, tp),
            P(cp, None),
        ),
        out_specs=(
            P(cp, None),
            P(cp, None),
            P(cp),
            P(),
            P(),
            P(cp, tp),
            P(cp, tp),
            P(cp, tp),
            P(cp, tp),
            P(cp),
            P(cp, None),
            P(cp, None, tp),
            P(cp, None, tp),
            P(cp, None, tp),
        ),
        check_vma=False,
    )
```

time: 2540 us -> 921 us (0.36)
  waiting for transfers between devices: 1850 us -> 0 us
  Pallas kernels: 0 us -> 649 us
  blocking collectives: 228 us -> 0 us
  matrix products: 194 us -> 45.5 us
    all_gather x18 -> x0, waiting for transfers between devices: 1130 us -> none  [the longest x2 243 us: gather_experts(): lax.all_gather(w_up, 'cp', axis=0, tiled=True)]
    pallas_call x0 -> x18, Pallas kernels: none -> 649 us  [the longest x16 630 us: exchange(): pl.pallas_call(kernel, out_shape=outs, in_specs=spaces, out_specs=spaces,...]
    reduce_scatter x5 -> x0, waiting for transfers between devices: 648 us -> none  [the longest x1 402 us: on_device(): lax.psum_scatter(jnp.concatenate([gate_term, up_term, down_term], axis=2)...]
    all_gather x7 -> x0, blocking collectives: 159 us -> none  [the longest x2 61.6 us: gather_experts(): lax.all_gather(w_router, 'cp', axis=0, tiled=True)]
    dot_general x73 -> x18, matrix products: 194 us -> 45.5 us  [dot(): return lax.dot_general(left, right, dims, preferred_element_type=f32)]
    psum x5 -> x0, waiting for transfers between devices: 65.6 us -> none  [the longest x1 34.3 us: forward_pass(): lax.psum(mixture_part.astype(jnp.bfloat16), 'tp').astype(jnp.float32)]
    psum x2 -> x0, blocking collectives: 45.8 us -> none  [the longest x1 40 us: on_device(): lax.psum((q_gain_term, k_gain_term), ('cp', 'tp'))]
    gather x6 -> x0, local copies, waits for them, and re-layouts: 32.7 us -> none  [the longest x2 8.47 us: forward_pass(): slot_inputs = normed_mid[token_of_slot].reshape(experts, CAP, -1)]
  transfers between devices with their start and end apart: 28 -> 0, of which waited for: 24 -> 0; matrix products, arithmetic and copies ran while one was open for 9% -> 0% of each run, Pallas kernels for 0% -> 0%
where the time goes in v1:
time: 921 us; the launch traced here: 910 us
  Pallas kernels  649 us (70%)
  local copies, waits for them, and re-layouts  124 us (13%)
  other arithmetic  90.3 us (10%)
  matrix products  45.5 us (5%)
    pallas_call x16, Pallas kernels, exchange(): pl.pallas_call(kernel, out_shape=outs, in_specs=spaces, out_specs=spaces,...  630 us
    dot_general x18, matrix products, dot(): return lax.dot_general(left, right, dims, preferred_element_type=f32)  45.5 us
    unnamed x210, local copies, waits for them, and re-layouts  39.6 us
    reduce_sum x2, other arithmetic, select(): jnp.sum(jnp.where((chosen[:, k:k + 1] == expert_range)[:, :, None], array...  20.9 us

profile of v1, /device:TPU:0, one launch (start us, length us, event | category | flops | bytes accessed | tf_op | source)
XLA Modules:
  0.0 910.5 jit_solution(2033490498829527884)
XLA Ops:
  7.3 34.2 %shard_map.263 = (bf16[4,256,512]{2,1,0:T(8,128)(2,1)}, bf16[2,256,512]{2,1,0:T(8,128)(2,1)}, bf16[2,256,512]{2,1,0:T(8,128)(2,1)}, bf16[2,256,512]{2,1,0:T(8,12...) custom-call(bf16[4,256,512]{2,1,0:T(8,128)(2,1)} %bitcast.361, ...), custom_call_target="tpu_custom_call" | custom-call | tf_op jit(solution)/shard_map/pallas_call | solution.py:98
  47.9 3.5 convolution_convert_fusion.3
  51.4 3.2 copy.334
  54.7 2.8 copy.335
  58.9 110.6 %shard_map.264 = (bf16[4,1024,384]{2,1,0:T(8,128)(2,1)}, bf16[2,256,512]{2,1,0:T(8,128)(2,1)}, bf16[2,256,8,256]{3,2,1,0:T(8,128)(2,1)}, bf16[2,256,8,256]{3,2,1...) custom-call(bf16[4,1024,384]{2,1,0:T(8,128)(2,1)} %bitcast.346, ...), custom_call_target="tpu_custom_call" | custom-call | tf_op jit(solution)/shard_map/pallas_call | solution.py:98
  169.5 2.5 convert_reduce_fusion
  175.5 1.9 multiply_cosine_fusion
  177.4 3.1 fusion.7
  184.1 22.8 %shard_map.265 = (bf16[2,1024,256]{2,1,0:T(8,128)(2,1)}, bf16[4,256,512]{2,1,0:T(8,128)(2,1)}) custom-call(bf16[1024,256]{1,0:T(8,128)(2,1)} %pad_maximum_fusion.6.refs_0_, bf16[4,256,512]{2,1,0:T(8,128)(2,1)} %bitcast.380), custom_call_target="tpu_custom_call" | custom-call | tf_op jit(solution)/shard_map/pallas_call | solution.py:98
  207.0 2.4 copy.398
  209.3 2.3 convolution_convert_fusion.2
  211.7 3.4 copy.399
  216.5 8.9 fusion.4
  229.8 7.4 shard_map.266
  237.1 49.7 %shard_map.267 = (bf16[4,1024,128]{2,1,0:T(8,128)(2,1)}, bf16[4,256,512]{2,1,0:T(8,128)(2,1)}) custom-call(bf16[1024,128]{1,0:T(8,128)(2,1)} %get-tuple-element.77.refs_0_, bf16[4,256,512]{2,1,0:T(8,128)(2,1)} %reshape.595.refs_1_), custom_call_target="tpu_custom_call" | custom-call | tf_op jit(solution)/shard_map/pallas_call | solution.py:98
  290.4 16.0 %shard_map.268 = bf16[4,256,512]{2,1,0:T(8,128)(2,1)} custom-call(bf16[4,256,512]{2,1,0:T(8,128)(2,1)} %bitcast.384), custom_call_target="tpu_custom_call" | custom-call | tf_op jit(solution)/shard_map/pallas_call | solution.py:98
  313.4 16.8 %shard_map.269 = (bf16[4,256,512]{2,1,0:T(8,128)(2,1)}, f32[4,16,256]{2,1,0:T(8,128)}) custom-call(bf16[256,512]{1,0:T(8,128)(2,1)} %multiply_convert_fusion.5.refs_0_, f32[16,256]{1,0:T(8,128)} %maximum_maximum_fusion.1.refs_1_), custom_call_target="tpu_custom_call" | custom-call | tf_op jit(solution)/shard_map/pallas_call | solution.py:98
  332.8 2.3 convolution_convert_fusion.1
  337.5 2.3 convolution_convert_fusion
  341.3 12.1 %fusion = (bf16[1024,256]{1,0:T(8,128)(2,1)S(1)}, bf16[1024,256]{1,0:T(8,128)(2,1)S(1)}, bf16[1024,256]{1,0:T(8,128)(2,1)S(1)}, bf16[1024,256]{1,0:T(8,128)(2,1)S(1)}) fusion(bf16[128,8,8,256]{3,2,1,0:T(8,128)(2,1)S(1)} %copy.403, pred[1024,8]{1,0:T(8,128)(4,1)S(1)} %iota_compare_fusion.1, pred[1024,8]{1,0:T(8,128)(4,1)S(1)} %iota_compare_fusion, ...), kind=kLoop, calls=%fused_computation.3 | loop fusion | flops 15728640 | bytes 10502144 | tf_op jit(solution)/shard_map/reduce_sum | solution.py:372
  353.6 3.5 copy.347
  357.1 4.4 reshape.606.refs_0_
  366.4 57.9 %shard_map.270 = (bf16[4,256,1024]{2,1,0:T(8,128)(2,1)}, f32[4,16,256]{2,1,0:T(8,128)}) custom-call(bf16[4,256,1024]{2,1,0:T(8,128)(2,1)} %reshape.606.refs_0_, f32[4,16,256]{2,1,0:T(8,128)} %reshape.608.refs_1_), custom_call_target="tpu_custom_call" | custom-call | tf_op jit(solution)/shard_map/pallas_call | solution.py:98
  427.0 3.0 convert_reduce_fusion.4
  430.1 2.5 copy.349
  432.6 2.5 copy.350
  435.2 2.4 broadcast_multiply_fusion
  438.5 2.0 copy.351
  440.6 2.0 copy.352
  442.6 1.9 multiply_reduce_fusion.6
  447.2 3.1 reshape.611.refs_0_
  450.3 58.1 %shard_map.271 = (bf16[4,256,1536]{2,1,0:T(8,128)(2,1)}, f32[4,8,256]{2,1,0:T(8,128)}) custom-call(bf16[256,1536]{1,0:T(8,128)(2,1)} %reshape.611.refs_0_, f32[8,256]{1,0:T(8,128)} %maximum_maximum_fusion.3.refs_1_), custom_call_target="tpu_custom_call" | custom-call | tf_op jit(solution)/shard_map/pallas_call | solution.py:98
  515.4 7.4 reshape.612
  522.8 3.6 fusion.54
  527.0 5.7 select_add_fusion
  534.3 2.4 convolution_convert_fusion.11
  539.4 2.4 fusion.60
  543.3 2.4 add_convert_fusion
  546.8 42.3 %shard_map.272 = (bf16[4,256,512]{2,1,0:T(8,128)(2,1)}, bf16[4,256,512]{2,1,0:T(8,128)(2,1)}, f32[4,16,256]{2,1,0:T(8,128)}) custom-call(bf16[4,256,512]{2,1,0:T(8,128)(2,1)} %bitcast.379, bf16[4,256,512]{2,1,0:T(8,128)(2,1)} %bitcast.378, f32[16,256]{1,0:T(8,128)} %maximum_maximum_fusion.2.refs_2_), custom_call_target="tpu_custom_call" | custom-call | tf_op jit(solution)/shard_map/pallas_call | solution.py:98
  597.0 2.9 fusion.52
  599.9 18.6 %shard_map.273 = (bf16[4,256,512]{2,1,0:T(8,128)(2,1)}, bf16[4,64,512]{2,1,0:T(8,128)(2,1)}) custom-call(bf16[256,512]{1,0:T(8,128)(2,1)} %get-tuple-element.235.refs_0_, bf16[4,64,512]{2,1,0:T(8,128)(2,1)} %fusion.12.refs_1_), custom_call_target="tpu_custom_call" | custom-call | tf_op jit(solution)/shard_map/pallas_call | solution.py:98
  623.3 2.3 copy.364
  626.9 24.3 %shard_map.274 = (bf16[4,1024,128]{2,1,0:T(8,128)(2,1)}, bf16[4,64,2048]{2,1,0:T(8,128)(2,1)}, f32[8,8,128]{2,1,0:T(8,128)}) custom-call(bf16[4,1024,128]{2,1,0:T(8,128)(2,1)} %bitcast.362, bf16[64,2048]{1,0:T(8,128)(2,1)} %bitcast.422, f32[8,128]{1,0:T(8,128)} %pad_bitcast_fusion.2.refs_2_), custom_call_target="tpu_custom_call" | custom-call | tf_op jit(solution)/shard_map/pallas_call | solution.py:98
  651.2 2.2 reduce_sum.502.cot_ref
  653.4 11.4 %shard_map.275 = (f32[1024,128]{1,0:T(8,128)}, f32[2048,256]{1,0:T(8,128)}) custom-call(bf16[1024,128]{1,0:T(8,128)(2,1)} %get-tuple-element.260.q_ref, bf16[2048,256]{1,0:T(8,128)(2,1)} %bitcast.360, s32[1024,1]{1,0:T(8,128)} %copy.342.dq_ref, s32[1,2048]{1,0:T(1,128)} %broadcast_in_dim_reshape.9.dk_ref, f32[1024,1]{1,0:T(8,128)} %get-tuple-element.97.norm_ref, ...), custom_call_target="tpu_custom_call" | custom-call | tf_op jit(solution)/shard_map/pallas_call | solution.py:222
  664.7 2.7 convert_element_type.271
  667.4 14.9 %shard_map.276 = bf16[2,1024,256]{2,1,0:T(8,128)(2,1)} custom-call(bf16[2,1024,256]{2,1,0:T(8,128)(2,1)} %bitcast.358), custom_call_target="tpu_custom_call" | custom-call | tf_op jit(solution)/shard_map/pallas_call | solution.py:98
  686.1 1.9 multiply_reduce_fusion.2
  688.6 3.8 convolution_convert_fusion.4
  692.3 3.8 convolution_convert_fusion.5
  696.1 3.8 convolution_convert_fusion.6
  700.9 106.6 %shard_map.277 = (bf16[4,1024,384]{2,1,0:T(8,128)(2,1)}, bf16[2,256,2048]{2,1,0:T(8,128)(2,1)}, bf16[2,256,2048]{2,1,0:T(8,128)(2,1)}, bf16[2,256,2048]{2,1,0:T(...) custom-call(bf16[1024,384]{1,0:T(8,128)(2,1)} %pad_maximum_fusion.3.refs_0_, bf16[2,256,2048]{2,1,0:T(8,128)(2,1)} %bitcast.410, ...), custom_call_target="tpu_custom_call" | custom-call | tf_op jit(solution)/shard_map/pallas_call | solution.py:98
  807.5 4.8 copy.368
  812.3 5.0 convolution_convert_fusion.7
  821.6 30.8 %shard_map.278 = (bf16[4,256,512]{2,1,0:T(8,128)(2,1)}, f32[4,8,128]{2,1,0:T(8,128)}, bf16[2,256,1536]{2,1,0:T(8,128)(2,1)}, bf16[2,256,512]{2,1,0:T(8,128)(2,1)...) custom-call(bf16[4,256,512]{2,1,0:T(8,128)(2,1)} %bitcast.377, f32[4,8,128]{2,1,0:T(8,128)} %bitcast.456, ...), custom_call_target="tpu_custom_call" | custom-call | tf_op jit(solution)/shard_map/pallas_call | solution.py:98
  852.4 3.0 convert_reduce_fusion.5
  858.3 2.0 copy.375
  860.4 2.1 copy.376
  866.7 10.4 %shard_map.279 = (bf16[4,64,512]{2,1,0:T(8,128)(2,1)}, f32[8,8,128]{2,1,0:T(8,128)}) custom-call(bf16[4,64,512]{2,1,0:T(8,128)(2,1)} %bitcast.437, f32[8,128]{1,0:T(8,128)} %pad_bitcast_fusion.1.refs_1_), custom_call_target="tpu_custom_call" | custom-call | tf_op jit(solution)/shard_map/pallas_call | solution.py:98
  878.8 15.8 %shard_map.280 = bf16[4,64,2048]{2,1,0:T(8,128)(2,1)} custom-call(bf16[64,2048]{1,0:T(8,128)(2,1)} %bitcast.423), custom_call_target="tpu_custom_call" | custom-call | tf_op jit(solution)/shard_map/pallas_call | solution.py:98
  894.6 2.9 bitcast_convert_fusion
  900.9 2.2 copy.411
  903.5 2.2 copy.412
  906.2 2.2 copy.413
  (353 shorter events, 107.9 us)
Async XLA Ops:
  2.9 2.9 copy-start.11
  4.5 2.2 copy-start.80
  41.5 3.2 copy-start.40
  42.3 2.3 copy-start.47
  43.0 1.6 copy-start.64
  43.1 2.1 copy-start.39
  44.7 2.1 copy-start.30
  54.6 2.8 copy-start.78
  54.6 3.6 copy-start.81
  169.5 2.9 copy-start.84
  169.5 3.5 copy-start.85
  172.4 1.9 copy-start.54
  172.5 1.9 copy-start.56
  177.4 3.1 copy-start.1
  177.4 3.1 copy-start.3
  206.9 2.4 copy-start.45
  209.3 2.4 copy-start.17
  211.7 3.4 copy-start.67
  225.5 2.6 copy-start.60
  237.1 51.2 %copy-start.82 = (bf16[2,256,512]{2,1,0:T(8,128)(2,1)S(1)}, bf16[2,256,512]{2,1,0:T(8,128)(2,1)}, u32[]{:S(2)}) copy-start(bf16[2,256,512]{2,1,0:T(8,128)(2,1)} %get-tuple-element.80) | copy-start | bytes 1572868
  290.4 17.4 %copy-start.73 = (f32[2,8,128]{2,1,0:T(8,128)S(1)}, f32[2,8,128]{2,1,0:T(8,128)}, u32[]{:S(2)}) copy-start(f32[2,8,128]{2,1,0:T(8,128)} %get-tuple-element.73) | copy-start | bytes 24580
  290.4 17.5 %copy-start = (bf16[4,256,512]{2,1,0:T(8,128)(2,1)S(1)}, bf16[4,256,512]{2,1,0:T(8,128)(2,1)}, u32[]{:S(2)}) copy-start(bf16[4,256,512]{2,1,0:T(8,128)(2,1)} %get-tuple-element.65) | copy-start | bytes 3145732
  306.4 2.3 copy-start.66
  307.9 23.8 %copy-start.58 = (f32[1,2,2,128]{3,1,2,0:T(2,128)}, f32[1,2,2,128]{3,1,2,0:T(2,128)S(1)}, u32[]{:S(2)}) copy-start(f32[1,2,2,128]{3,1,2,0:T(2,128)S(1)} %copy.395) | copy-start | bytes 6148
  330.2 1.9 copy-start.20
  331.7 5.8 copy-start.12
  332.8 2.4 copy-start.21
  335.2 1.6 copy-start.19
  337.5 2.4 copy-start.23
  435.2 2.4 copy-start.32
  442.6 2.7 copy-start.44
  532.7 1.6 copy-start.18
  534.2 2.4 copy-start.5
  539.3 2.5 copy-start.7
  541.7 1.6 copy-start.24
  543.3 2.4 copy-start.9
  592.4 2.4 copy-start.33
  592.4 3.3 copy-start.41
  619.9 1.7 copy-start.83
  621.6 4.0 copy-start.42
  621.6 4.7 copy-start.72
  667.4 16.5 %copy-start.4 = (f32[1024,64]{1,0:T(8,128)S(1)}, f32[1024,64]{1,0:T(8,128)}, u32[]{:S(2)}) copy-start(f32[1024,64]{1,0:T(8,128)} %copy-done.3) | copy-start | bytes 786436
  685.2 3.4 copy-start.6
  686.0 2.6 copy-start.46
  688.6 3.8 copy-start.10
  688.6 3.8 copy-start.13
  692.3 3.8 copy-start.8
  807.5 4.8 copy-start.31
  812.3 5.0 copy-start.14
  812.3 5.0 copy-start.29
  819.2 1.9 copy-start.70
  860.4 4.5 copy-start.48
  860.4 5.4 copy-start.69
  860.4 5.5 copy-start.16
  860.4 5.5 copy-start.65
  878.8 18.8 %copy-start.62 = (f32[8,8,128]{2,1,0:T(8,128)S(1)}, f32[8,8,128]{2,1,0:T(8,128)}, u32[]{:S(2)}) copy-start(f32[8,8,128]{2,1,0:T(8,128)} %get-tuple-element.107) | copy-start | bytes 98308
  878.8 19.4 %copy-start.37 = (bf16[2,256,512]{2,1,0:T(8,128)(2,1)S(1)}, bf16[2,256,512]{2,1,0:T(8,128)(2,1)}, u32[]{:S(2)}) copy-start(bf16[2,256,512]{2,1,0:T(8,128)(2,1)} %get-tuple-element.110) | copy-start | bytes 1572868
  894.6 4.5 copy-start.68
  894.6 5.2 copy-start.61
  894.6 5.8 copy-start.27
  900.9 2.2 copy-start.26
  903.5 2.2 copy-start.25
  906.2 2.2 copy-start.59
  906.2 2.8 copy-start.36
  (22 other events, 22.8 us)

commit v2 on v1

v2 whole, which is shorter than its diff:
```python
import functools
import types

import jax
import jax.numpy as jnp
import numpy as np
from jax import lax
from jax.experimental import pallas as pl
from jax.experimental.pallas import tpu as pltpu
from jax.sharding import Mesh
from jax.sharding import PartitionSpec as P

eps = 1e-05
theta = 50000.0
negative = -1e30
AXES = ("b", "a", "y", "c")
MESH = pl.DeviceIdType.MESH
bf16 = jnp.bfloat16
f32 = jnp.float32


NT = (((1,), (1,)), ((), ()))
TN = (((0,), (0,)), ((), ()))


def dot(left, right, dims=(((1,), (0,)), ((), ()))):
    return lax.dot_general(left, right, dims, preferred_element_type=f32)


class Net:
    def __init__(self, sizes, send, recv):
        self.sizes, self.send, self.recv, self.used = sizes, send, recv, 0
        self.me = {axis: lax.axis_index(axis) for axis in AXES}

    def near(self, **offs):
        return {axis: lax.rem(self.me[axis] + off, self.sizes[axis]) for axis, off in offs.items()}

    def copy(self, source, target, place):
        slot = self.used
        self.used += 1
        return pltpu.make_async_remote_copy(
            src_ref=source,
            dst_ref=target,
            send_sem=self.send.at[slot],
            recv_sem=self.recv.at[slot],
            device_id=place,
            device_id_type=MESH,
        )

    def greet(self, places):
        barrier = pltpu.get_barrier_semaphore()
        for place in places:
            pl.semaphore_signal(barrier, inc=1, device_id=place, device_id_type=MESH)
        pl.semaphore_wait(barrier, len(places))

    def pick(self, *values):
        result = values[-1]
        for i in range(len(values) - 2, -1, -1):
            result = jnp.where(self.me["b"] == i, values[i], result)
        return result

    def reduce(self, *args):
        return Reduce(self, *args)

    def spread(self, *blocks):
        return Spread(self, blocks)


class Reduce:
    def __init__(self, net, parts, got, make=None):
        self.net, self.parts, self.got = net, parts, got
        self.b = b = net.me["b"]
        self.base = net.used
        net.used += 4
        self.order = [3 - b, net.pick(2, 0, 3, 1), net.pick(1, 3, 0, 2)]
        for k in range(2):
            if make is not None:
                make(self.order[k])
            self.hop(self.order[k]).start()
        if make is not None:
            make(self.order[2])

    def hop(self, d):
        net, b = self.net, self.b
        far = ((b == 0) & (d == 3)) | ((b == 3) & (d == 0))
        beside = jnp.where(b == 0, 1, 2)
        target, slot = jnp.where(far, beside, d), jnp.where(far, beside, b)
        return pltpu.make_async_remote_copy(
            src_ref=self.parts.at[d],
            dst_ref=self.got.at[slot],
            send_sem=net.send.at[self.base + d],
            recv_sem=net.recv.at[self.base + slot],
            device_id={"b": target},
            device_id_type=MESH,
        )

    def came(self, i):
        net = self.net
        return pltpu.make_async_remote_copy(
            src_ref=self.got.at[i],
            dst_ref=self.got.at[i],
            send_sem=net.send.at[self.base + i],
            recv_sem=net.recv.at[self.base + i],
            device_id=net.near(b=1),
            device_id_type=MESH,
        )

    def inner(self):
        b, d = self.b, self.order[2]

        @pl.when((b == 1) | (b == 2))
        def _():
            self.came(b).wait_recv()
            rows = self.parts.shape[1]
            step = 256 if rows % 256 == 0 else rows

            @pl.loop(0, rows // step)
            def _(i):
                sl = pl.ds(pl.multiple_of(i * step, step), step)
                total = self.parts[d, sl, :].astype(f32) + self.got[b, sl, :].astype(f32)
                self.parts[d, sl, :] = total.astype(bf16)

        self.hop(d).start()

    def wait(self):
        for i in range(4):

            @pl.when((self.b != i) & (jnp.abs(self.b - i) <= 2))
            def _():
                self.came(i).wait_recv()

    def total(self, *index):
        b = self.b
        value = self.parts[(b,) + index].astype(f32)
        for i in range(4):
            valid = (b != i) & (jnp.abs(b - i) <= 2)
            value = value + jnp.where(valid, self.got[(i,) + index].astype(f32), 0.0)
        return value

    def finish(self):
        for d in range(4):

            @pl.when(self.b != d)
            def _():
                self.hop(d).wait_send()


class Spread:
    def __init__(self, net, blocks):
        self.net, self.blocks = net, blocks
        self.b = b = net.me["b"]
        self.base = net.used
        net.used += 4 * len(blocks)
        self.targets = [net.pick(2, 3, 0, 1), net.pick(1, 0, 3, 2), net.pick(2, 2, 1, 1)]
        self.order = [net.pick(1, 3, 0, 2), net.pick(2, 0, 3, 1), net.pick(3, 2, 1, 0)]
        self.inner = (b == 1) | (b == 2)
        for k, target in enumerate(self.targets):
            if k < 2:
                for j in range(len(blocks)):
                    self.hop(b, target, target, j).start()
            else:

                @pl.when(self.inner)
                def _():
                    for j in range(len(blocks)):
                        self.hop(b, target, target, j).start()

    def hop(self, i, target, slot, j):
        net, count = self.net, len(self.blocks)
        return pltpu.make_async_remote_copy(
            src_ref=self.blocks[j](i),
            dst_ref=self.blocks[j](i),
            send_sem=net.send.at[self.base + slot * count + j],
            recv_sem=net.recv.at[self.base + i * count + j],
            device_id={"b": target},
            device_id_type=MESH,
        )

    def take(self, i):
        b = self.b
        onward = ((b == 1) & (i == 3)) | ((b == 2) & (i == 0))
        for j in range(len(self.blocks)):
            self.hop(i, self.net.near(b=1)["b"], b, j).wait_recv()

            @pl.when(onward)
            def _():
                self.hop(i, jnp.where(b == 1, 0, 3), b, j).start()

    def take_all(self):
        for i in self.order:
            self.take(i)

    def finish(self):
        b = self.b
        for k, target in enumerate(self.targets):
            for j in range(len(self.blocks)):
                if k < 2:
                    self.hop(b, target, target, j).wait_send()
                else:

                    @pl.when(self.inner)
                    def _():
                        self.hop(b, target, target, j).wait_send()
                        self.hop(b, jnp.where(b == 1, 0, 3), b, j).wait_send()


def rope(values, cos_tab, sin_tab):
    return values * cos_tab + pltpu.roll(values, values.shape[1] // 2, 1) * sin_tab


def head_norm(values):
    return lax.rsqrt(jnp.mean(values * values, axis=1, keepdims=True) + eps)


def unrope(grad, raw, gain, cos_tab, sin_tab):
    factor = head_norm(raw)
    normed = raw * factor
    turned = grad * cos_tab + pltpu.roll(grad * sin_tab, grad.shape[1] // 2, 1)
    gain_part = jnp.sum(turned * normed, axis=0, keepdims=True)
    inner = turned * gain
    slope = jnp.mean(raw * inner, axis=1, keepdims=True)
    return factor * inner - raw * (factor * factor * factor * slope), gain_part


class TwoLevel:
    def __init__(self, net, acc, sendc, recvc, sendy, recvy, used):
        self.net, self.acc = net, acc
        self.sendc, self.recvc, self.sendy, self.recvy = sendc, recvc, sendy, recvy
        self.used = used
        self.base = net.used
        net.used += 16
        self.part = acc.shape[2]
        self.half = acc.shape[1]

    def lane(self, j):
        return slice(j * self.part, (j + 1) * self.part)

    def hop(self, i, j, level):
        net = self.net
        source, target = ((self.sendc, self.recvc), (self.sendy, self.recvy))[level]
        slot = self.base + 8 * level + 2 * i + j
        lane = pl.ds(j * self.part, self.part)
        return pltpu.make_async_remote_copy(
            src_ref=source.at[i, :, lane],
            dst_ref=target.at[i, :, lane],
            send_sem=net.send.at[slot],
            recv_sem=net.recv.at[slot],
            device_id=net.near(c=1) if level == 0 else net.near(y=1),
            device_id_type=MESH,
        )

    def put(self, i, j, term, k):
        first = self.net.me["c"] == 0
        low, high = term[: self.half], term[self.half :]
        self.acc[k] = jnp.where(first, low, high)
        self.sendc[i, :, self.lane(j)] = jnp.where(first, high, low).astype(bf16)
        self.hop(i, j, 0).start()

    def onward(self, i, j, k):
        self.hop(i, j, 0).wait_recv()
        total = self.acc[k] + self.recvc[i, :, self.lane(j)].astype(f32)
        self.sendy[i, :, self.lane(j)] = total.astype(bf16)
        self.hop(i, j, 1).start()

    def total(self, i, j):
        self.hop(i, j, 1).wait_recv()
        lane = self.lane(j)
        return self.sendy[i, :, lane].astype(f32) + self.recvy[i, :, lane].astype(f32)

    def finish(self):
        for i in range(4):
            for j in range(self.used):
                self.hop(i, j, 0).wait_send()
                self.hop(i, j, 1).wait_send()


def transpose_columns(columns, rows):
    lane = lax.broadcasted_iota(jnp.int32, (rows, 128), 1)
    table = jnp.zeros((rows, 128), f32)
    for k, column in enumerate(columns):
        table = jnp.where(lane == k, column, table)
    return jnp.transpose(table)[:8, :]


INS = (
    "tok", "cot", "wq_in", "wk_in", "wv_in", "wo_in", "wg_in", "wu_in", "wd_in", "ids_in",
    "docs_in", "router_in", "gain_in_a", "gain_in_f", "gain_q", "gain_k", "speed_in",
)
OUTS = (
    "out_rows", "in_rows", "gate_own", "up_own", "down_own", "gate_in", "up_in", "down_in",
    "proj_out", "tail",
)
WORK = (
    "xc", "cotc", "rows_all", "rows_own", "cols_own", "cols_all", "cols_sum", "wqkv", "wo",
    "wg", "wu", "wd", "stage", "hn", "raw", "q_rot", "kv", "stat", "ho", "cos_tab", "sin_tab",
    "pkv", "gkv", "pq", "gq", "pcd", "gcd", "acc", "sendc", "recvc", "sendy", "recvy", "hidden", "scaled",
    "small", "small_in", "pay", "wide", "pair", "late_small", "extra_own", "extra_in", "d_attn",
    "out_half", "block_out", "head_acc", "dkv_acc", "dkv_send", "dkv_in", "gsend", "gin_w",
    "gout", "gout_in", "gin", "s4", "gain_acc", "tail_all", "gains", "ids", "docs", "proj",
    "send", "recv", "local",
)


def layer_kernel(sizes, dims, *refs):
    r = types.SimpleNamespace(**dict(zip(INS + OUTS + WORK, refs)))
    nb, na, head, heads, experts, ff, top = dims
    net = Net(sizes, r.send, r.recv)
    me = net.me
    b, a, y, c = me["b"], me["a"], me["y"], me["c"]
    tok, part = r.xc.shape[1], r.xc.shape[2]
    half, col, model, width, sub = tok // 2, nb * tok, nb * part, heads * head, part // na
    scale = head**-0.5
    mine = pl.ds(pl.multiple_of(c * half, half), half)
    own_lane = pl.ds(pl.multiple_of(b * part, part), part)
    head_lane = pl.ds(pl.multiple_of(b * head, head), head)
    core, across = net.near(c=1), net.near(y=1)
    b_peers = [net.near(b=k) for k in range(1, nb)]
    a_peers = [net.near(a=k) for k in range(1, na)]
    ab_peers = [net.near(b=j, a=k) for j in range(nb) for k in range(na) if j or k]
    group = [
        net.near(b=i, y=j, c=k)
        for i in range(nb) for j in range(2) for k in range(2) if i or j or k
    ]
    tp_peers = [net.near(y=j, c=k) for j in range(2) for k in range(2) if j or k]
    sent = []
    local_used = [0]

    def rows_of(i):
        return pl.ds(pl.multiple_of(i * tok, tok), tok)

    def lane_of(place):
        return pl.ds(pl.multiple_of(place * part, part), part)

    def move(source, target):
        copy = pltpu.make_async_copy(source, target, r.local.at[local_used[0]])
        local_used[0] += 1
        copy.start()
        return copy

    def ship(source, target, place):
        copy = net.copy(source, target, place)
        copy.start()
        sent.append(copy)
        return copy

    def arrive(copies):
        for copy in copies:
            copy.wait_recv()

    def drain(copies):
        for copy in copies:
            copy.wait_send()
            sent[:] = [other for other in sent if other is not copy]

    tok_here = move(r.tok, r.gin)
    w_here = [move(w, r.wqkv.at[j, a]) for j, w in ((1, r.wk_in), (2, r.wv_in), (0, r.wq_in))]
    stage_copy = move(r.wd_in, r.stage)
    late_here = [move(r.wo_in, r.wo.at[a]), move(r.cot.at[:, own_lane], r.cotc.at[b])]
    net.greet(group + [net.near(b=j, a=k) for j in range(nb) for k in range(1, na)])

    r.cols_own[...] = jnp.zeros_like(r.cols_own)
    r.cols_own[0:experts, :] = r.router_in[...].astype(f32)
    r.cols_own[experts : experts + 1, :] = r.gain_in_a[...].astype(f32)
    r.cols_own[experts + 1 : experts + 2, :] = r.gain_in_f[...].astype(f32)
    r.gains[0:1, :] = r.gain_q[...].astype(f32)
    r.gains[1:2, :] = r.gain_k[...].astype(f32)
    r.gains[2:3, :] = r.speed_in[...]
    r.rows_own[...] = jnp.zeros_like(r.rows_own)
    r.rows_own[1 : 1 + top, :] = r.ids_in[...].astype(f32)
    r.rows_own[3:4, :] = r.docs_in[...].astype(f32)

    exchange = [net.pick(2, 3, 0, 1), net.pick(3, 2, 1, 0), net.pick(1, 0, 3, 2)]

    def to_quarters(source, target):
        return [
            ship(source.at[mine, lane_of(d)], target.at[b, mine, :], {"b": d}) for d in exchange
        ]

    def over_a(source, target):
        return [ship(source, target.at[a], place) for place in a_peers]

    def to_core(copies, target):
        more = []
        for source_b, copy in zip(exchange, copies):
            copy.wait_recv()
            block = target.at[source_b, mine, :]
            more.append(ship(block, block, core))
        return more

    x_copies = to_quarters(r.tok, r.xc)
    cols_copies = over_a(r.cols_own, r.cols_all)
    r.cols_all[a] = r.cols_own[...]
    kv_weights = over_a(r.wk_in, r.wqkv.at[1]) + over_a(r.wv_in, r.wqkv.at[2])
    q_weights = over_a(r.wq_in, r.wqkv.at[0])
    tok_here.wait()
    square_columns = []
    for s in range(tok // 64):
        piece = r.gin[s * 64 : (s + 1) * 64, :].astype(f32)
        square_columns.append(jnp.sum(piece * piece, axis=1, keepdims=True))
    squares = transpose_columns([jnp.concatenate(square_columns, axis=0)], tok)[0:1, :]
    which8 = lax.broadcasted_iota(jnp.int32, (8, tok), 0)
    r.rows_own[0:1, :] = lax.rsqrt(squares / model + eps)
    rows_copies = [ship(r.rows_own, r.rows_all.at[a, b], place) for place in ab_peers]
    r.rows_all[a, b] = r.rows_own[...]
    r.xc[b] = r.gin[:, own_lane]
    cot_copies = to_quarters(r.cot, r.cotc)
    wo_copies = over_a(r.wo_in, r.wo)

    def relayout(target):
        step = 32

        @pl.loop(0, sub // step)
        def _(n):
            rows = pl.ds(pl.multiple_of(n * step, step), step)
            turned = jnp.swapaxes(r.stage[rows].astype(f32), 0, 1)
            for e in range(experts):
                target[a, rows, e * ff : (e + 1) * ff] = turned[e].astype(bf16)

    stage_copy.wait()
    relayout(r.wd)
    wd_copies = over_a(r.wd.at[a], r.wd)
    stage_copy = move(r.wg_in, r.stage)

    lane_index = lax.broadcasted_iota(jnp.int32, (tok, head), 1)
    row_index = lax.broadcasted_iota(jnp.int32, (tok, head), 0)

    @pl.loop(0, nb)
    def _(i):
        place = ((i * na + a) * tok + row_index).astype(f32)
        angle = place * r.gains[2:3, :]
        r.cos_tab[rows_of(i), :] = jnp.cos(angle)
        turned = jnp.sin(angle)
        r.sin_tab[rows_of(i), :] = jnp.where(lane_index < head // 2, -turned, turned)

    x_more = to_core(x_copies, r.xc)
    arrive(rows_copies + cols_copies + x_more)
    arrive(kv_weights)
    for copy in w_here:
        copy.wait()
    for k in range(na):
        r.cols_sum[:, k * sub : (k + 1) * sub] = r.cols_all[k]
    gain_in = r.cols_sum[experts : experts + 1, :]
    for i in range(nb):
        columns = jnp.transpose(r.rows_all[a, i])
        r.ids[i] = columns
        r.hn[i] = (r.xc[i].astype(f32) * columns[:, 0:1] * gain_in).astype(bf16)
        for j in range(na):
            r.docs[j, :, i * tok : (i + 1) * tok] = r.rows_all[j, i][3:4, :]

    def weight(j):
        return r.wqkv[j].reshape(part, width)

    @pl.loop(0, nb)
    def _(i):
        for j in (1, 2):
            term = dot(r.hn[i], weight(j)).astype(bf16)
            for h in range(heads):
                piece = term[:, h * head : (h + 1) * head]
                r.pkv[h, rows_of(i), (j - 1) * head : j * head] = piece

    kv_sum = net.reduce(r.pkv, r.gkv)
    arrive(q_weights)

    @pl.loop(0, nb)
    def _(i):
        term = dot(r.hn[i], weight(0)).astype(bf16)
        for h in range(heads):
            r.pq[h, rows_of(i), :] = term[:, h * head : (h + 1) * head]

    stage_copy.wait()
    relayout(r.wg)
    wg_copies = over_a(r.wg.at[a], r.wg)
    stage_copy = move(r.wu_in, r.stage)
    kv_sum.inner()
    q_sum = net.reduce(r.pq, r.gq)
    stage_copy.wait()
    relayout(r.wu)
    q_sum.inner()
    cot_more = to_core(cot_copies, r.cotc)
    kv_sum.wait()

    @pl.loop(0, nb)
    def _(i):
        rows = rows_of(i)
        both = kv_sum.total(rows)
        r.raw[rows, head:] = both
        keys = both[:, :head]
        normed = keys * head_norm(keys) * r.gains[1:2, :]
        r.kv[a, rows, :head] = rope(normed, r.cos_tab[rows, :], r.sin_tab[rows, :]).astype(bf16)
        r.kv[a, rows, head:] = both[:, head:].astype(bf16)

    kv_copies = over_a(r.kv.at[a], r.kv)
    wu_copies = over_a(r.wu.at[a], r.wu)
    arrive(wd_copies + cot_more)
    for copy in late_here:
        copy.wait()

    def chosen(left, weights, d, put):
        columns = r.ids[d]
        values = [jnp.zeros((tok, ff), f32) for k in range(top)]
        for e in range(experts):
            term = dot(left, weights[:, :, e * ff : (e + 1) * ff].reshape(part, ff))
            for k in range(top):
                values[k] = jnp.where(columns[:, 1 + k : 2 + k] == e, term, values[k])
        for k in range(top):
            put(k, values[k].astype(bf16))

    groups = ff // head

    @pl.loop(0, nb)
    def _(i):
        def put(k, value):
            for g in range(groups):
                r.pcd[k, i, g * tok : (g + 1) * tok, :] = value[:, g * head : (g + 1) * head]

        chosen(r.cotc[i], r.wd, i, put)

    cd_sums = [net.reduce(r.pcd.at[0], r.gcd.at[0])]
    q_sum.wait()

    @pl.loop(0, nb)
    def _(i):
        rows = rows_of(i)
        query = q_sum.total(rows)
        r.raw[rows, :head] = query
        normed = query * head_norm(query) * r.gains[0:1, :]
        r.q_rot[rows, :] = rope(normed, r.cos_tab[rows, :], r.sin_tab[rows, :]).astype(bf16)

    cd_sums[0].inner()

    def attend(block, first, last):
        @pl.loop(0, nb)
        def _(i):
            rows = rows_of(i)
            columns = r.ids[i]
            scores = dot(r.q_rot[rows, :], r.kv[block, :, :head], NT) * scale
            scores = jnp.where(columns[:, 3:4] == r.docs[block], scores, negative)
            most = jnp.max(scores, axis=1, keepdims=True)
            if not first:
                before = r.stat[rows, 0:1]
                most = jnp.maximum(before, most)
            terms = jnp.exp(scores - most)
            total = jnp.sum(terms, axis=1, keepdims=True)
            mixed = dot(terms.astype(bf16), r.kv[block, :, head:])
            if not first:
                fade = jnp.exp(before - most)
                total = r.stat[rows, 1:2] * fade + total
                mixed = r.head_acc[rows, :] * fade + mixed
            if last:
                r.ho[rows, head_lane] = (mixed * (1.0 / total)).astype(bf16)
                r.stat[rows, 2:3] = most + jnp.log(total)
            else:
                r.stat[rows, 0:1] = most
                r.stat[rows, 1:2] = total
                r.head_acc[rows, :] = mixed

    attend(a, True, na == 1)
    for k in range(1, na):
        kv_copies[k - 1].wait_recv()
        attend(lax.rem(a + na - k, na), False, k == na - 1)

    def head_block(array, i, start, size):
        return array.at[pl.ds(start, size), pl.ds(pl.multiple_of(i * head, head), head)]

    cuts = [0, nb - 1, nb]

    def ho_half(s):
        start, size = cuts[s] * tok, (cuts[s + 1] - cuts[s]) * tok
        return net.spread(lambda i: head_block(r.ho, i, start, size))

    ho_lines = [ho_half(0)]
    arrive(wo_copies)
    ho_lines[0].take(ho_lines[0].order[0])
    ho_lines.append(ho_half(1))

    mixer = TwoLevel(net, r.acc, r.sendc, r.recvc, r.sendy, r.recvy, 1)
    for s in range(2):
        if s == 0:
            ho_lines[0].take(ho_lines[0].order[1])
            ho_lines[0].take(ho_lines[0].order[2])
        else:
            ho_lines[1].take_all()
            for k in range(1, top):
                cd_sums.append(net.reduce(r.pcd.at[k], r.gcd.at[k]))
        for i in range(cuts[s], cuts[s + 1]):
            term = dot(r.ho[i * tok : (i + 1) * tok, :], r.wo[...].reshape(part, width), NT)
            mixer.put(i, 0, term, i)
        for i in range(cuts[s], cuts[s + 1]):
            mixer.onward(i, 0, i)
    for group_sum in cd_sums[1:]:
        group_sum.inner()
    gain_mid = r.cols_sum[experts + 1 : experts + 2, :]
    router = r.cols_sum[...].astype(bf16)
    last_copies = []
    for i in range(nb):
        value = r.xc[i, mine, :].astype(f32) + mixer.total(i, 0)
        r.hidden[i] = value
        piece = (value * gain_mid).astype(bf16)
        r.scaled[i, mine, :] = piece
        logits = dot(router, piece, NT)
        squares = jnp.sum(value * value, axis=1, keepdims=True)
        squares = jnp.transpose(jnp.broadcast_to(squares, (half, 128)))[:1, :]
        which = lax.broadcasted_iota(jnp.int32, logits.shape, 0)
        r.small[i, :, mine] = jnp.where(which == experts, squares, logits)
        for array in (r.scaled.at[i, mine, :], r.small.at[i, :, mine]):
            last_copies.append(ship(array, array, core))
    arrive(wg_copies + wu_copies + last_copies)
    mixer.finish()
    kv_sum.finish()
    q_sum.finish()

    small_copies = [ship(r.small.at[p["b"]], r.small_in.at[b], p) for p in b_peers]
    r.small_in[b] = r.small[b]

    def make(d):
        for j, w in enumerate((r.wg, r.wu)):

            def put(k, value, j=j):
                r.pkv[d, (2 * k + j) * tok : (2 * k + j + 1) * tok, :] = value

            chosen(r.scaled[d], w, d, put)

    gu_sum = net.reduce(r.pkv, r.gkv, make)
    gu_sum.inner()
    make(b)
    arrive(small_copies)
    for group_sum in cd_sums:
        group_sum.wait()
    gu_sum.wait()
    total = jnp.sum(r.small_in[...], axis=0)
    r_mid = lax.rsqrt(total[experts : experts + 1] / model + eps)
    logits = total[:experts] * r_mid
    terms = jnp.exp(logits - jnp.max(logits, axis=0, keepdims=True))
    probs = terms / jnp.sum(terms, axis=0, keepdims=True)
    which = lax.broadcasted_iota(jnp.int32, probs.shape, 0).astype(f32)
    picks = [r.rows_own[1 + k : 2 + k] == which for k in range(top)]
    combine = [jnp.sum(jnp.where(pick, probs, 0.0), axis=0, keepdims=True) for pick in picks]
    table = jnp.where(which8 == 0, r_mid, 0.0)
    for k in range(top):
        table = jnp.where(which8 == 1 + k, combine[k], table)
    columns = jnp.transpose(table)
    r_col = columns[:, 0:1]
    columns_back = []
    inner = jnp.zeros((tok, 1), f32)
    for k in range(top):
        gate = gu_sum.total(slice((2 * k) * tok, (2 * k + 1) * tok)) * r_col
        up = gu_sum.total(slice((2 * k + 1) * tok, (2 * k + 2) * tok)) * r_col
        back = jnp.concatenate(
            [
                cd_sums[k].total(slice(g * tok, (g + 1) * tok))
                for g in range(groups)
            ],
            axis=1,
        )
        sig = 1.0 / (1.0 + jnp.exp(-gate))
        silu = gate * sig
        act = silu * up
        weighed = columns[:, 1 + k : 2 + k]
        d_act = weighed * back
        d_gate = d_act * up * (sig * (1.0 + gate * (1.0 - sig)))
        d_up = d_act * silu
        for j, value in enumerate((weighed * act, d_gate * r_col, d_up * r_col)):
            r.pay[b, :, (top * j + k) * ff : (top * j + k + 1) * ff] = value.astype(bf16)
        columns_back.append(jnp.sum(act * back, axis=1, keepdims=True))
        inner = inner + jnp.sum(d_gate * gate + d_up * up, axis=1, keepdims=True)

    pay_line = net.spread(lambda i: r.pay.at[i])
    rank = y * sizes["c"] + c
    r.pair[rank] = transpose_columns(columns_back + [inner], tok)
    arrive([ship(r.pair.at[rank], r.pair.at[rank], place) for place in tp_peers])
    sums = r.pair[0] + r.pair[1] + r.pair[2] + r.pair[3]
    d_probs = jnp.zeros_like(probs)
    for k in range(top):
        d_probs = d_probs + jnp.where(picks[k], sums[k : k + 1], 0.0)
    d_logits = probs * (d_probs - jnp.sum(probs * d_probs, axis=0, keepdims=True))
    inner_row = sums[top : top + 1] + jnp.sum(d_logits * logits, axis=0, keepdims=True)
    r.late_small[b, 0:8, :] = d_logits * r_mid
    r.late_small[b, 8:16, :] = jnp.broadcast_to(r_mid * r_mid * inner_row / model, (8, tok))
    late_copies = [ship(r.late_small.at[b], r.late_small.at[b], place) for place in b_peers]

    mixer = TwoLevel(net, r.acc, r.sendc, r.recvc, r.sendy, r.recvy, 2)
    pieces = experts * ff // width
    by_piece = width // ff

    def expand(j, i, e):
        columns = r.ids[i]
        value = jnp.zeros((tok, ff), f32)
        for k in range(top):
            taken = r.pay[i, :, (top * j + k) * ff : (top * j + k + 1) * ff].astype(f32)
            value = jnp.where(columns[:, 1 + k : 2 + k] == e, taken, value)
        return value.astype(bf16)

    def use(i):
        def widen(j):
            for e in range(experts):
                g, h = e // by_piece, e % by_piece
                r.wide[j, g * tok : (g + 1) * tok, h * ff : (h + 1) * ff] = expand(j, i, e)

        def times(j, w):
            total = 0.0
            for g in range(pieces):
                piece = w[:, :, g * width : (g + 1) * width].reshape(part, width)
                total = total + dot(r.wide[j, g * tok : (g + 1) * tok, :], piece, NT)
            return total

        widen(1)
        widen(2)
        mixer.put(i, 0, times(1, r.wg) + times(2, r.wu), 0)
        widen(0)
        mixer.onward(i, 0, 0)
        mixer.put(i, 1, times(0, r.wd), 1)
        mixer.onward(i, 1, 1)

    @pl.loop(0, nb)
    def _(n):
        index = b
        for k in range(nb - 1):
            index = jnp.where(n == k + 1, pay_line.order[k], index)

        @pl.when(n > 0)
        def _():
            pay_line.take(index)

        use(index)

    arrive(late_copies)
    which16 = lax.broadcasted_iota(jnp.int32, (16, tok), 0)
    ffn_part = jnp.zeros((1, part), f32)
    attn_copies = []
    for i in range(nb):
        columns = jnp.transpose(r.late_small[i, :, mine])
        d_log = jnp.where(which16[:, :half] < experts, r.late_small[i, :, mine], 0.0).astype(bf16)
        mid = mixer.total(i, 0) + dot(d_log, router, TN)
        value = r.hidden[i]
        grad = r.cotc[i, mine, :].astype(f32) + gain_mid * mid - value * columns[:, 8:9]
        r.d_attn[i, mine, :] = grad.astype(bf16)
        attn_copies.append(ship(r.d_attn.at[i, mine, :], r.d_attn.at[i, mine, :], core))
        ffn_part = ffn_part + jnp.sum(mid * value, axis=0, keepdims=True)
        mix = mixer.total(i, 1)
        r.out_half[i] = (value + mix).astype(bf16)
        r.hidden[i] = grad
    d_hidden = r.hidden
    arrive(attn_copies)

    @pl.loop(0, nb)
    def _(i):
        term = dot(r.d_attn[i], r.wo[...].reshape(part, width)).astype(bf16)
        for h in range(heads):
            r.pq[h, rows_of(i), :] = term[:, h * head : (h + 1) * head]

    heads_sum = net.reduce(r.pq, r.gq)

    drain(wd_copies + wg_copies + wu_copies)
    gu_sum.finish()

    def to_a(source, target):
        return [ship(source.at[p["a"]], target.at[k], p) for k, p in enumerate(a_peers)]

    def expert_grad(j, left, target):
        @pl.loop(0, experts)
        def _(e):
            for i in range(nb):
                r.pkv[0, i * tok : (i + 1) * tok, :] = expand(j, i, e)
            grad = dot(left[...].reshape(col, part), r.pkv[0], TN).astype(bf16)
            lane = pl.ds(pl.multiple_of(e * ff, ff), ff)
            for k in range(na):
                target[k, :, lane] = grad[k * sub : (k + 1) * sub, :]

    expert_grad(0, r.cotc, r.wd)
    pending = to_a(r.wd, r.down_in)
    results = [move(r.wd.at[a], r.down_own)]
    heads_sum.inner()
    term = dot(r.d_attn[...].reshape(col, part), r.ho[...], TN).astype(bf16)
    r.gout[...] = term.reshape(na, sub, width)
    extra = 0.0
    for i in range(nb):
        d_log = jnp.where(which16 < experts, r.late_small[i], 0.0).astype(bf16)
        extra = extra + dot(d_log, r.scaled[i])
    which_row = lax.broadcasted_iota(jnp.int32, (16, part), 0)
    r.extra_own[...] = jnp.where(which_row == experts + 1, ffn_part, extra)
    expert_grad(1, r.scaled, r.wg)
    heads_sum.wait()
    out_copies = [
        ship(r.out_half.at[p["b"]], r.block_out.at[mine, own_lane], p) for p in b_peers
    ]
    r.block_out[mine, own_lane] = r.out_half[b]

    r.gain_acc[...] = jnp.zeros_like(r.gain_acc)

    @pl.loop(0, nb)
    def _(i):
        rows = rows_of(i)
        cot = heads_sum.total(rows).astype(bf16)
        r.pq[b, rows, :] = cot
        delta = jnp.sum(cot.astype(f32) * r.ho[rows, head_lane].astype(f32), axis=1, keepdims=True)
        r.stat[rows, 4:5] = delta

    def attend_back(block, first, last, start, stop):
        @pl.loop(start, stop)
        def _(i):
            rows = rows_of(i)
            columns = r.ids[i]
            query, cot = r.q_rot[rows, :], r.pq[b, rows, :]
            keys, values = r.kv[block, :, :head], r.kv[block, :, head:]
            scores = dot(query, keys, NT) * scale
            keep = columns[:, 3:4] == r.docs[block]
            probs = jnp.where(keep, jnp.exp(scores - r.stat[rows, 2:3]), 0.0)
            d_scores = (probs * (dot(cot, values, NT) - r.stat[rows, 4:5])).astype(bf16)
            key_term = dot(d_scores, query, TN) * scale
            value_term = dot(probs.astype(bf16), cot, TN)

            @pl.when(i == 0)
            def _():
                r.dkv_acc[:, :head] = key_term
                r.dkv_acc[:, head:] = value_term

            @pl.when(i > 0)
            def _():
                r.dkv_acc[:, :head] += key_term
                r.dkv_acc[:, head:] += value_term

            grad = dot(d_scores, keys) * scale
            if not first:
                grad = r.head_acc[rows, :] + grad
            if not last:
                r.head_acc[rows, :] = grad
            else:
                source = r.raw[rows, :head]
                grad, gain_part = unrope(
                    grad, source, r.gains[0:1, :], r.cos_tab[rows, :], r.sin_tab[rows, :]
                )
                r.gain_acc[0:1, :] += gain_part
                r.wide[0, rows, head_lane] = grad.astype(bf16)
                r.stat[rows, 3:4] = jnp.sum(grad * source, axis=1, keepdims=True)

    kv_back = []
    for k in range(1, na):
        attend_back(lax.rem(a + k, na), k == 1, False, 0, nb)
        r.dkv_send[k - 1] = r.dkv_acc[...].astype(bf16)
        kv_back.append(ship(r.dkv_send.at[k - 1], r.dkv_in.at[k - 1], a_peers[k - 1]))
    pending += to_a(r.wg, r.gate_in) + to_a(r.gout, r.gout_in)
    results.append(move(r.wg.at[a], r.gate_own))
    q_lines = []
    for s in range(2):
        attend_back(a, na == 1, True, s * (nb // 2), (s + 1) * (nb // 2))
        q_lines.append(
            net.spread(lambda i, s=s: head_block(r.wide.at[0], i, s * (col // 2), col // 2))
        )
    out_more = []
    for k, copy in zip(range(1, nb), out_copies):
        lane = lane_of(lax.rem(b + nb - k, nb))
        copy.wait_recv()
        out_more.append(ship(r.block_out.at[mine, lane], r.block_out.at[mine, lane], core))
    out_more.append(ship(r.block_out.at[mine, own_lane], r.block_out.at[mine, own_lane], core))
    expert_grad(2, r.scaled, r.wu)
    pending += to_a(r.wu, r.up_in)
    results.append(move(r.wu.at[a], r.up_own))
    arrive(kv_back)

    @pl.loop(0, nb)
    def _(i):
        rows = rows_of(i)
        both = r.dkv_acc[rows, :]
        for k in range(na - 1):
            both = both + r.dkv_in[k, rows, :].astype(f32)
        source = r.raw[rows, head : 2 * head]
        grad, gain_part = unrope(
            both[:, :head], source, r.gains[1:2, :], r.cos_tab[rows, :], r.sin_tab[rows, :]
        )
        r.gain_acc[1:2, :] += gain_part
        value_grad = both[:, head:]
        r.wide[1, rows, head_lane] = grad.astype(bf16)
        r.wide[2, rows, head_lane] = value_grad.astype(bf16)
        r.stat[rows, 3:4] += jnp.sum(
            grad * source + value_grad * r.raw[rows, 2 * head :], axis=1, keepdims=True
        )

    def kv_half(s):
        start, size = cuts[s] * tok, (cuts[s + 1] - cuts[s]) * tok
        return net.spread(
            lambda i: head_block(r.wide.at[1], i, start, size),
            lambda i: head_block(r.wide.at[2], i, start, size),
        )

    for line in q_lines:
        line.take(line.order[0])
    kv_lines = [kv_half(0)]
    place16 = (b * 2 + y) * 2 + c
    r.s4[place16] = transpose_columns([r.stat[i * tok : (i + 1) * tok, 3:4] for i in range(nb)], tok)
    r.s4[place16, 4:6, 0:head] = r.gain_acc[0:2, :]
    s4_copies = [ship(r.s4.at[place16], r.s4.at[place16], place) for place in group]

    def weight_grad(j):
        grad = dot(r.hn[...].reshape(col, part), r.wide[j], TN).astype(bf16)
        r.gsend[j] = grad.reshape(na, sub, width)
        return to_a(r.gsend.at[j], r.gin_w.at[j])

    for line in q_lines:
        line.take(line.order[1])
        line.take(line.order[2])
    pending += weight_grad(0)
    kv_lines[0].take(kv_lines[0].order[0])
    kv_lines.append(kv_half(1))

    mixer_in = TwoLevel(net, r.acc, r.sendc, r.recvc, r.sendy, r.recvy, 1)
    mixer.finish()
    arrive(s4_copies)
    for s in range(2):
        if s == 0:
            kv_lines[0].take(kv_lines[0].order[1])
            kv_lines[0].take(kv_lines[0].order[2])
        else:
            kv_lines[1].take_all()
        for i in range(cuts[s], cuts[s + 1]):
            rows = slice(i * tok, (i + 1) * tok)
            term = dot(r.wide[0, rows, :], weight(0), NT)
            term = term + dot(r.wide[1, rows, :], weight(1), NT)
            mixer_in.put(i, 0, term + dot(r.wide[2, rows, :], weight(2), NT), i)
        for i in range(cuts[s], cuts[s + 1]):
            mixer_in.onward(i, 0, i)
    sums = r.s4[0]
    for k in range(1, 4 * nb):
        sums = sums + r.s4[k]
    inner_columns = jnp.transpose(sums)
    attn_part = jnp.zeros((1, part), f32)
    in_hops = []
    base_in = net.used
    net.used += nb

    def in_hop(d, slot):
        return pltpu.make_async_remote_copy(
            src_ref=r.out_half.at[d],
            dst_ref=r.gin.at[mine, own_lane],
            send_sem=r.send.at[base_in + d],
            recv_sem=r.recv.at[base_in + slot],
            device_id={"b": jnp.int32(d)},
            device_id_type=MESH,
        )

    drain(out_copies)
    for i in range(nb):
        d_in = mixer_in.total(i, 0)
        r_col = r.ids[i, mine, 0:1]
        inner = jnp.where(
            c == 0, inner_columns[:half, i : i + 1], inner_columns[half:, i : i + 1]
        )
        x = r.xc[i, mine, :].astype(f32)
        scaled = d_in * r_col
        grad = d_hidden[i] + scaled * gain_in - x * (r_col * r_col * inner / model)
        attn_part = attn_part + jnp.sum(scaled * x, axis=0, keepdims=True)
        r.out_half[i] = grad.astype(bf16)

        @pl.when(b == i)
        def _():
            r.gin[mine, own_lane] = r.out_half[i]

        @pl.when(b != i)
        def _():
            in_hop(i, b).start()

    r.extra_own[...] = jnp.where(which_row == experts + 2, attn_part, r.extra_own[...])
    tail_copy = ship(r.extra_own, r.extra_in, core)
    pending += weight_grad(1)
    pending += weight_grad(2)
    tail_copy.wait_recv()
    shared = (which_row == experts + 1) | (which_row == experts + 2)
    r.tail_all[a] = r.extra_own[...] + jnp.where(shared, r.extra_in[...], 0.0)
    r.tail_all[a, experts + 3 : experts + 5, 0:head] = sums[4:6, 0:head]
    tail_copies = over_a(r.tail_all.at[a], r.tail_all)
    in_more = []
    for k in range(1, nb):
        place = lax.rem(b + k, nb)
        lane = lane_of(place)
        pltpu.make_async_remote_copy(
            src_ref=r.gin.at[mine, lane],
            dst_ref=r.gin.at[mine, lane],
            send_sem=r.send.at[base_in + place],
            recv_sem=r.recv.at[base_in + place],
            device_id=core,
            device_id_type=MESH,
        ).wait_recv()
        in_more.append(ship(r.gin.at[mine, lane], r.gin.at[mine, lane], core))
    in_more.append(ship(r.gin.at[mine, own_lane], r.gin.at[mine, own_lane], core))
    arrive(out_more)
    results.append(move(r.block_out, r.out_rows))
    arrive(pending)
    for j in range(4):
        mine_here = r.gsend[j, a] if j < 3 else r.gout[a]
        total = mine_here.astype(f32)
        for k in range(na - 1):
            came = r.gin_w[j, k] if j < 3 else r.gout_in[k]
            total = total + came.astype(f32)
        r.proj[j] = total
    results.append(move(r.proj, r.proj_out))
    arrive(tail_copies)
    r.tail[...] = jnp.sum(r.tail_all[...], axis=0)
    arrive(in_more)
    results.append(move(r.gin, r.in_rows))
    mixer_in.finish()
    for line in [heads_sum, pay_line] + cd_sums + ho_lines + q_lines + kv_lines:
        line.finish()
    for d in range(nb):

        @pl.when(b != d)
        def _():
            in_hop(d, b).wait_send()

    drain(list(sent))
    for copy in results:
        copy.wait()
    assert net.used <= r.send.shape[0] and local_used[0] <= r.local.shape[0]


def layer(sizes, dims, ins):
    nb, na, head, heads, experts, ff, top = dims
    tok, model = ins[0].shape
    part, col, half = model // nb, nb * tok, tok // 2
    sub, width, wide = part // na, heads * head, experts * ff
    others = max(na - 1, 1)
    shape = jax.ShapeDtypeStruct
    vmem, hbm = pl.BlockSpec(memory_space=pltpu.VMEM), pl.BlockSpec(memory_space=pl.ANY)
    outs = [
        shape((tok, model), bf16),
        shape((tok, model), bf16),
        shape((sub, wide), bf16),
        shape((sub, wide), bf16),
        shape((sub, wide), bf16),
        shape((others, sub, wide), bf16),
        shape((others, sub, wide), bf16),
        shape((others, sub, wide), bf16),
        shape((4, sub, width), f32),
        shape((16, part), f32),
    ]
    work = dict(
        xc=((nb, tok, part), bf16),
        cotc=((nb, tok, part), bf16),
        rows_all=((na, nb, 8, tok), f32),
        rows_own=((8, tok), f32),
        cols_own=((16, sub), f32),
        cols_all=((na, 16, sub), f32),
        cols_sum=((16, part), f32),
        wqkv=((3, na, sub, width), bf16),
        wo=((na, sub, width), bf16),
        wg=((na, sub, wide), bf16),
        wu=((na, sub, wide), bf16),
        wd=((na, sub, wide), bf16),
        stage=((sub, experts, ff), bf16),
        hn=((nb, tok, part), bf16),
        raw=((col, 3 * head), f32),
        q_rot=((col, head), bf16),
        kv=((na, col, 2 * head), bf16),
        stat=((col, 128), f32),
        ho=((col, width), bf16),
        cos_tab=((col, head), f32),
        sin_tab=((col, head), f32),
        pkv=((nb, col, 2 * head), bf16),
        gkv=((nb, col, 2 * head), bf16),
        pq=((nb, col, head), bf16),
        gq=((nb, col, head), bf16),
        pcd=((top, nb, ff // head * tok, head), bf16),
        gcd=((top, nb, ff // head * tok, head), bf16),
        acc=((nb, half, part), f32),
        sendc=((nb, half, 2 * part), bf16),
        recvc=((nb, half, 2 * part), bf16),
        sendy=((nb, half, 2 * part), bf16),
        recvy=((nb, half, 2 * part), bf16),
        hidden=((nb, half, part), f32),
        scaled=((nb, tok, part), bf16),
        small=((nb, 16, tok), f32),
        small_in=((nb, 16, tok), f32),
        pay=((nb, tok, 3 * top * ff), bf16),
        wide=((3, col, width), bf16),
        pair=((4, 8, tok), f32),
        late_small=((nb, 16, tok), f32),
        extra_own=((16, part), f32),
        extra_in=((16, part), f32),
        d_attn=((nb, tok, part), bf16),
        out_half=((nb, half, part), bf16),
        block_out=((tok, model), bf16),
        head_acc=((col, head), f32),
        dkv_acc=((col, 2 * head), f32),
        dkv_send=((others, col, 2 * head), bf16),
        dkv_in=((others, col, 2 * head), bf16),
        gsend=((3, na, sub, width), bf16),
        gin_w=((3, others, sub, width), bf16),
        gout=((na, sub, width), bf16),
        gout_in=((others, sub, width), bf16),
        gin=((tok, model), bf16),
        s4=((4 * nb, 8, tok), f32),
        gain_acc=((8, head), f32),
        tail_all=((na, 16, part), f32),
        ids=((nb, tok, 8), f32),
        gains=((8, head), f32),
        docs=((na, 1, col), f32),
        proj=((4, sub, width), f32),
    )
    count = 160 + 26 * na
    scratch = [pltpu.VMEM(*work[name]) for name in WORK[:-3]] + [
        pltpu.SemaphoreType.DMA((count,)),
        pltpu.SemaphoreType.DMA((count,)),
        pltpu.SemaphoreType.DMA((24,)),
    ]
    return pl.pallas_call(
        functools.partial(layer_kernel, sizes, dims),
        out_shape=outs,
        in_specs=[hbm] * 9 + [vmem] * 8,
        out_specs=[hbm] * 9 + [vmem],
        scratch_shapes=scratch,
        compiler_params=pltpu.CompilerParams(
            collective_id=1, has_side_effects=True, vmem_limit_bytes=67043328
        ),
        name="layer",
    )(*ins)


def last_kernel(experts, ff, sub, *refs):
    out_rows, in_rows, owns, cames, proj = refs[0], refs[1], refs[2:5], refs[5:8], refs[8]
    tail, refs = refs[9], refs[10:]
    block_out, grad_in, grads, projections = refs[0], refs[1], refs[2:5], refs[5:9]
    router, gain_attn, gain_ffn, gain_q, gain_k = refs[9:]
    block_out[...] = out_rows[...]
    grad_in[...] = in_rows[...].astype(f32)
    for own, came, grad in zip(owns, cames, grads):
        for e in range(experts):
            lane = slice(e * ff, (e + 1) * ff)
            total = own[:, lane].astype(f32)
            for k in range(came.shape[0]):
                total = total + came[k, :, lane].astype(f32)
            grad[:, e, :] = total
    for j in range(4):
        projections[j][...] = proj[j]

    @pl.when(pl.program_id(0) == 0)
    def _():
        a = lax.axis_index("a")
        piece = tail[:, :sub]
        for k in range(1, tail.shape[1] // sub):
            piece = jnp.where(a == k, tail[:, k * sub : (k + 1) * sub], piece)
        router[...] = piece[:experts]
        gain_ffn[...] = piece[experts + 1 : experts + 2]
        gain_attn[...] = piece[experts + 2 : experts + 3]
        gain_q[...] = tail[experts + 3 : experts + 4, : gain_q.shape[1]]
        gain_k[...] = tail[experts + 4 : experts + 5, : gain_k.shape[1]]


def last(dims, ins):
    nb, na, head, heads, experts, ff, top = dims
    tok, model = ins[0].shape
    sub, wide = ins[2].shape
    others, width = ins[5].shape[0], ins[8].shape[2]
    steps = 4
    shape = jax.ShapeDtypeStruct
    rows = pl.BlockSpec((tok // steps, model), lambda i: (i, 0))
    own = pl.BlockSpec((sub // steps, wide), lambda i: (i, 0))
    came = pl.BlockSpec((others, sub // steps, wide), lambda i: (0, i, 0))
    grad = pl.BlockSpec((sub // steps, experts, ff), lambda i: (i, 0, 0))
    flat = pl.BlockSpec((sub // steps, width), lambda i: (i, 0))
    small = [shape((experts, sub), f32), shape((1, sub), f32), shape((1, sub), f32)]
    small += [shape((1, head), f32)] * 2
    return pl.pallas_call(
        functools.partial(last_kernel, experts, ff, sub),
        grid=(steps,),
        out_shape=[shape((tok, model), bf16), shape((tok, model), f32)]
        + [shape((sub, experts, ff), f32)] * 3
        + [shape((sub, width), f32)] * 4
        + small,
        in_specs=[rows, rows] + [own] * 3 + [came] * 3
        + [pl.BlockSpec((4, sub // steps, width), lambda i: (0, i, 0))]
        + [pl.BlockSpec(ins[9].shape, lambda i: (0, 0))],
        out_specs=[rows, rows] + [grad] * 3 + [flat] * 4
        + [pl.BlockSpec(item.shape, lambda i: (0, 0)) for item in small],
        name="last",
    )(*ins)


def on_device(
    sizes,
    tokens_in,
    doc_ids,
    expert_ids,
    attn_gain,
    q_gain,
    k_gain,
    w_query,
    w_key,
    w_value,
    w_output,
    ffn_gain,
    w_router,
    w_gate,
    w_up,
    w_down,
    cotangent,
):
    nb, na = sizes["b"], sizes["a"]
    tok, model = tokens_in.shape
    part = model // nb
    sub = part // na
    head = q_gain.shape[0]
    width = w_query.shape[1]
    heads = width // head
    experts, ff = w_gate.shape[1], w_gate.shape[2]
    top = expert_ids.shape[1]
    dims = (nb, na, head, heads, experts, ff, top)

    speed = theta ** (-2.0 * (np.arange(head) % (head // 2)) / head)
    parts = layer(
        sizes,
        dims,
        [
            tokens_in, cotangent, w_query, w_key, w_value, w_output, w_gate, w_up, w_down,
            expert_ids.T, doc_ids[None], w_router.T, attn_gain[None], ffn_gain[None], q_gain[None],
            k_gain[None], jnp.asarray(speed, f32)[None],
        ],
    )
    (
        block_out, grad_in, grad_gate, grad_up, grad_down, grad_query, grad_key, grad_value,
        grad_output, router, gain_attn, gain_ffn, gain_q, gain_k,
    ) = last(dims, parts)
    return (
        block_out,
        grad_in,
        gain_attn.reshape(sub),
        gain_q.reshape(head),
        gain_k.reshape(head),
        grad_query,
        grad_key,
        grad_value,
        grad_output,
        gain_ffn.reshape(sub),
        router.T,
        grad_gate,
        grad_up,
        grad_down,
    )


def solution(mesh):
    cp, tp = mesh.shape["cp"], mesh.shape["tp"]
    sizes = {"b": 4, "a": cp // 4, "y": 2, "c": tp // 2}
    split = Mesh(mesh.devices.reshape([sizes[axis] for axis in AXES]), AXES)
    cp, tp = ("b", "a"), ("y", "c")
    return jax.shard_map(
        functools.partial(on_device, sizes),
        mesh=split,
        in_specs=(
            P(cp, None),
            P(cp),
            P(cp, None),
            P(cp),
            P(),
            P(),
            P(cp, tp),
            P(cp, tp),
            P(cp, tp),
            P(cp, tp),
            P(cp),
            P(cp, None),
            P(cp, None, tp),
            P(cp, None, tp),
            P(cp, None, tp),
            P(cp, None),
        ),
        out_specs=(
            P(cp, None),
            P(cp, None),
            P(cp),
            P(),
            P(),
            P(cp, tp),
            P(cp, tp),
            P(cp, tp),
            P(cp, tp),
            P(cp),
            P(cp, None),
            P(cp, None, tp),
            P(cp, None, tp),
            P(cp, None, tp),
        ),
        check_vma=False,
    )
```

time: 921 us -> 357 us (0.39); the launches traced: 910 us -> 357 us
  Pallas kernels: 649 us -> 354 us
  local copies, waits for them, and re-layouts: 124 us -> 2.44 us
  other arithmetic: 90.3 us -> 0 us
  matrix products: 45.5 us -> 0 us
    pallas_call x18 -> x2, Pallas kernels: 649 us -> 354 us  [the longest x1 345 us: layer(): pl.pallas_call(functools.partial(layer_kernel, sizes, dims), out_shape=ou...]
    reduce_sum x36 -> x0, other arithmetic: 53.2 us -> none  [the longest x2 20.9 us: select(): jnp.sum(jnp.where((chosen[:, k:k + 1] == expert_range)[:, :, None], array...]
    reshape x32 -> x0, local copies, waits for them, and re-layouts: 47.2 us -> none  [the longest x1 7.39 us: on_device(): pay_all = got[0].reshape(col, 3, top, ff)]
    dot_general x18 -> x0, matrix products: 45.5 us -> none  [dot(): return lax.dot_general(left, right, dims, preferred_element_type=f32)]
    unnamed x210 -> x0, local copies, waits for them, and re-layouts: 39.6 us -> none
    convert_element_type x12 -> x0, other arithmetic: 13.6 us -> none  [the longest x1 3.05 us: on_device(): kv_own = jnp.concatenate([k_rot.astype(bf16), v_raw.astype(bf16)], axis=1)]
where the time goes in v2:
time: 357 us
  Pallas kernels  354 us (99%)
    pallas_call x1, Pallas kernels, layer(): pl.pallas_call(functools.partial(layer_kernel, sizes, dims), out_shape=ou...  345 us
    pallas_call x1, Pallas kernels, last(): pl.pallas_call(functools.partial(last_kernel, experts, ff, sub), grid=(st...  9.15 us

profile of v2, /device:TPU:0, one launch (start us, length us, event | category | flops | bytes accessed | tf_op | source)
XLA Modules:
  0.0 357.0 jit_solution(11989142250839482955)
XLA Ops:
  0.6 1.2 broadcast_in_dim.19.refs_12_
  1.9 1.2 broadcast_in_dim.20.refs_13_
  3.1 344.6 %layer.1 = (bf16[256,2048]{1,0:T(8,128)(2,1)}, bf16[256,2048]{1,0:T(8,128)(2,1)}, bf16[256,2048]{1,0:T(8,128)(2,1)}, bf16[256,2048]{1,0:T(8,128)(2,1)}, bf16[256...) custom-call(bf16[256,2048]{1,0:T(8,128)(2,1)} %refs_0_.1, ...), custom_call_target="tpu_custom_call" | custom-call | tf_op jit(solution)/shard_map/layer/pallas_call | solution.py:1103
  347.7 9.1 %last.1 = (bf16[256,2048]{1,0:T(8,128)(2,1)}, f32[256,2048]{1,0:T(8,128)}, f32[256,8,256]{2,1,0:T(8,128)}, f32[256,8,256]{2,1,0:T(8,128)}, f32[256,8,256]{2,1,0:...) custom-call(bf16[256,2048]{1,0:T(8,128)(2,1)} %get-tuple-element.38., ...), custom_call_target="tpu_custom_call" | custom-call | tf_op jit(solution)/shard_map/last/pallas_call | solution.py:1160

commit v3 on v2

--- a/solution.py
+++ b/solution.py
@@ -62,8 +62,8 @@
     def reduce(self, *args):
         return Reduce(self, *args)
 
-    def spread(self, *blocks):
-        return Spread(self, blocks)
+    def spread(self, *blocks, start=True):
+        return Spread(self, blocks, start)
 
 
 class Reduce:
@@ -146,7 +146,7 @@
 
 
 class Spread:
-    def __init__(self, net, blocks):
+    def __init__(self, net, blocks, start):
         self.net, self.blocks = net, blocks
         self.b = b = net.me["b"]
         self.base = net.used
@@ -154,16 +154,31 @@
         self.targets = [net.pick(2, 3, 0, 1), net.pick(1, 0, 3, 2), net.pick(2, 2, 1, 1)]
         self.order = [net.pick(1, 3, 0, 2), net.pick(2, 0, 3, 1), net.pick(3, 2, 1, 0)]
         self.inner = (b == 1) | (b == 2)
+        if start:
+            self.begin()
+
+    def begin(self):
         for k, target in enumerate(self.targets):
             if k < 2:
-                for j in range(len(blocks)):
-                    self.hop(b, target, target, j).start()
+                for j in range(len(self.blocks)):
+                    self.hop(self.b, target, target, j).start()
             else:
 
                 @pl.when(self.inner)
                 def _():
-                    for j in range(len(blocks)):
-                        self.hop(b, target, target, j).start()
+                    for j in range(len(self.blocks)):
+                        self.hop(self.b, target, target, j).start()
+
+    def after(self, other):
+        @pl.when(jnp.logical_not(self.inner))
+        def _():
+            self.begin()
+
+        other.take(other.order[0])
+
+        @pl.when(self.inner)
+        def _():
+            self.begin()
 
     def hop(self, i, target, slot, j):
         net, count = self.net, len(self.blocks)
@@ -293,7 +308,7 @@
 WORK = (
     "xc", "cotc", "rows_all", "rows_own", "cols_own", "cols_all", "cols_sum", "wqkv", "wo",
     "wg", "wu", "wd", "stage", "hn", "raw", "q_rot", "kv", "stat", "ho", "cos_tab", "sin_tab",
-    "pkv", "gkv", "pq", "gq", "pcd", "gcd", "acc", "sendc", "recvc", "sendy", "recvy", "hidden", "scaled",
+    "pkv", "gkv", "pq", "gq", "pcd", "gcd", "acc", "sendc", "recvc", "sendy", "recvy", "hidden", "d_hidden", "scaled",
     "small", "small_in", "pay", "wide", "pair", "late_small", "extra_own", "extra_in", "d_attn",
     "out_half", "block_out", "head_acc", "dkv_acc", "dkv_send", "dkv_in", "gsend", "gin_w",
     "gout", "gout_in", "gin", "s4", "gain_acc", "tail_all", "gains", "ids", "docs", "proj",
@@ -316,7 +331,6 @@
     core, across = net.near(c=1), net.near(y=1)
     b_peers = [net.near(b=k) for k in range(1, nb)]
     a_peers = [net.near(a=k) for k in range(1, na)]
-    ab_peers = [net.near(b=j, a=k) for j in range(nb) for k in range(na) if j or k]
     group = [
         net.near(b=i, y=j, c=k)
         for i in range(nb) for j in range(2) for k in range(2) if i or j or k
@@ -360,8 +374,8 @@
 
     r.cols_own[...] = jnp.zeros_like(r.cols_own)
     r.cols_own[0:experts, :] = r.router_in[...].astype(f32)
-    r.cols_own[experts : experts + 1, :] = r.gain_in_a[...].astype(f32)
-    r.cols_own[experts + 1 : experts + 2, :] = r.gain_in_f[...].astype(f32)
+    r.cols_own[experts : experts + 1, :] = r.gain_in_a[...].astype(f32).reshape(1, sub)
+    r.cols_own[experts + 1 : experts + 2, :] = r.gain_in_f[...].astype(f32).reshape(1, sub)
     r.gains[0:1, :] = r.gain_q[...].astype(f32)
     r.gains[1:2, :] = r.gain_k[...].astype(f32)
     r.gains[2:3, :] = r.speed_in[...]
@@ -371,20 +385,24 @@
 
     exchange = [net.pick(2, 3, 0, 1), net.pick(3, 2, 1, 0), net.pick(1, 0, 3, 2)]
 
+    quarter = half // 2
+    fourth = pl.ds(pl.multiple_of(c * half + y * quarter, quarter), quarter)
+
     def to_quarters(source, target):
         return [
-            ship(source.at[mine, lane_of(d)], target.at[b, mine, :], {"b": d}) for d in exchange
+            ship(source.at[fourth, lane_of(d)], target.at[b, fourth, :], {"b": d})
+            for d in exchange
         ]
 
     def over_a(source, target):
         return [ship(source, target.at[a], place) for place in a_peers]
 
-    def to_core(copies, target):
+    def onward(copies, target, rows, place):
         more = []
         for source_b, copy in zip(exchange, copies):
             copy.wait_recv()
-            block = target.at[source_b, mine, :]
-            more.append(ship(block, block, core))
+            block = target.at[source_b, rows, :]
+            more.append(ship(block, block, place))
         return more
 
     x_copies = to_quarters(r.tok, r.xc)
@@ -400,7 +418,11 @@
     squares = transpose_columns([jnp.concatenate(square_columns, axis=0)], tok)[0:1, :]
     which8 = lax.broadcasted_iota(jnp.int32, (8, tok), 0)
     r.rows_own[0:1, :] = lax.rsqrt(squares / model + eps)
-    rows_copies = [ship(r.rows_own, r.rows_all.at[a, b], place) for place in ab_peers]
+    rows_copies = [ship(r.rows_own, r.rows_all.at[a, b], place) for place in b_peers]
+    rows_far = [
+        ship(r.rows_own, r.rows_all.at[a, b], net.near(b=j, a=k))
+        for j in range(nb) for k in range(1, na)
+    ]
     r.rows_all[a, b] = r.rows_own[...]
     r.xc[b] = r.gin[:, own_lane]
     cot_copies = to_quarters(r.cot, r.cotc)
@@ -432,7 +454,8 @@
         turned = jnp.sin(angle)
         r.sin_tab[rows_of(i), :] = jnp.where(lane_index < head // 2, -turned, turned)
 
-    x_more = to_core(x_copies, r.xc)
+    x_y = onward(x_copies, r.xc, fourth, across)
+    x_more = onward(x_y, r.xc, mine, core)
     arrive(rows_copies + cols_copies + x_more)
     arrive(kv_weights)
     for copy in w_here:
@@ -444,8 +467,6 @@
         columns = jnp.transpose(r.rows_all[a, i])
         r.ids[i] = columns
         r.hn[i] = (r.xc[i].astype(f32) * columns[:, 0:1] * gain_in).astype(bf16)
-        for j in range(na):
-            r.docs[j, :, i * tok : (i + 1) * tok] = r.rows_all[j, i][3:4, :]
 
     def weight(j):
         return r.wqkv[j].reshape(part, width)
@@ -459,6 +480,7 @@
                 r.pkv[h, rows_of(i), (j - 1) * head : j * head] = piece
 
     kv_sum = net.reduce(r.pkv, r.gkv)
+    cot_y = onward(cot_copies, r.cotc, fourth, across)
     arrive(q_weights)
 
     @pl.loop(0, nb)
@@ -469,14 +491,19 @@
 
     stage_copy.wait()
     relayout(r.wg)
-    wg_copies = over_a(r.wg.at[a], r.wg)
+    low, high = (pl.ds(k * experts * ff // 2, experts * ff // 2) for k in range(2))
+
+    def half_over_a(array, lane):
+        return [ship(array.at[a, :, lane], array.at[a, :, lane], place) for place in a_peers]
+
+    wg_copies = half_over_a(r.wg, low)
     stage_copy = move(r.wu_in, r.stage)
     kv_sum.inner()
     q_sum = net.reduce(r.pq, r.gq)
     stage_copy.wait()
     relayout(r.wu)
     q_sum.inner()
-    cot_more = to_core(cot_copies, r.cotc)
+    cot_more = onward(cot_y, r.cotc, mine, core)
     kv_sum.wait()
 
     @pl.loop(0, nb)
@@ -490,6 +517,7 @@
         r.kv[a, rows, head:] = both[:, head:].astype(bf16)
 
     kv_copies = over_a(r.kv.at[a], r.kv)
+    wg_copies += half_over_a(r.wg, high)
     wu_copies = over_a(r.wu.at[a], r.wu)
     arrive(wd_copies + cot_more)
     for copy in late_here:
@@ -516,6 +544,10 @@
         chosen(r.cotc[i], r.wd, i, put)
 
     cd_sums = [net.reduce(r.pcd.at[0], r.gcd.at[0])]
+    arrive(rows_far)
+    for i in range(nb):
+        for j in range(na):
+            r.docs[j, :, i * tok : (i + 1) * tok] = r.rows_all[j, i][3:4, :]
     q_sum.wait()
 
     @pl.loop(0, nb)
@@ -527,6 +559,14 @@
         r.q_rot[rows, :] = rope(normed, r.cos_tab[rows, :], r.sin_tab[rows, :]).astype(bf16)
 
     cd_sums[0].inner()
+
+    deep = 2 if na <= 2 else 1
+
+    def deep_rows(i):
+        return pl.ds(pl.multiple_of(i * deep * tok, deep * tok), deep * tok)
+
+    def deep_ids(i):
+        return r.ids[pl.ds(i * deep, deep)].reshape(deep * tok, 8)
 
     def attend(block, first, last):
         @pl.loop(0, nb)
@@ -566,12 +606,12 @@
 
     def ho_half(s):
         start, size = cuts[s] * tok, (cuts[s + 1] - cuts[s]) * tok
-        return net.spread(lambda i: head_block(r.ho, i, start, size))
+        return net.spread(lambda i: head_block(r.ho, i, start, size), start=s == 0)
 
     ho_lines = [ho_half(0)]
     arrive(wo_copies)
-    ho_lines[0].take(ho_lines[0].order[0])
     ho_lines.append(ho_half(1))
+    ho_lines[1].after(ho_lines[0])
 
     mixer = TwoLevel(net, r.acc, r.sendc, r.recvc, r.sendy, r.recvy, 1)
     for s in range(2):
@@ -664,7 +704,8 @@
         columns_back.append(jnp.sum(act * back, axis=1, keepdims=True))
         inner = inner + jnp.sum(d_gate * gate + d_up * up, axis=1, keepdims=True)
 
-    pay_line = net.spread(lambda i: r.pay.at[i])
+    pay_line = net.spread(lambda i: r.pay.at[i, :, pl.ds(top * ff, 2 * top * ff)])
+    act_line = net.spread(lambda i: r.pay.at[i, :, pl.ds(0, top * ff)], start=False)
     rank = y * sizes["c"] + c
     r.pair[rank] = transpose_columns(columns_back + [inner], tok)
     arrive([ship(r.pair.at[rank], r.pair.at[rank], place) for place in tp_peers])
@@ -706,10 +747,7 @@
         widen(1)
         widen(2)
         mixer.put(i, 0, times(1, r.wg) + times(2, r.wu), 0)
-        widen(0)
         mixer.onward(i, 0, 0)
-        mixer.put(i, 1, times(0, r.wd), 1)
-        mixer.onward(i, 1, 1)
 
     @pl.loop(0, nb)
     def _(n):
@@ -721,8 +759,31 @@
         def _():
             pay_line.take(index)
 
+        @pl.when(n == jnp.where(act_line.inner, 1, 2))
+        def _():
+            act_line.begin()
+
         use(index)
 
+    drain(wd_copies + wg_copies + wu_copies)
+    gu_sum.finish()
+
+    def to_a(source, target):
+        return [ship(source.at[p["a"]], target.at[k], p) for k, p in enumerate(a_peers)]
+
+    def expert_grad(j, left, target):
+        @pl.loop(0, experts)
+        def _(e):
+            for i in range(nb):
+                r.pkv[0, i * tok : (i + 1) * tok, :] = expand(j, i, e)
+            grad = dot(left[...].reshape(col, part), r.pkv[0], TN).astype(bf16)
+            lane = pl.ds(pl.multiple_of(e * ff, ff), ff)
+            for k in range(na):
+                target[k, :, lane] = grad[k * sub : (k + 1) * sub, :]
+
+    expert_grad(1, r.scaled, r.wg)
+    pending = to_a(r.wg, r.gate_in)
+    results = [move(r.wg.at[a], r.gate_own)]
     arrive(late_copies)
     which16 = lax.broadcasted_iota(jnp.int32, (16, tok), 0)
     ffn_part = jnp.zeros((1, part), f32)
@@ -736,10 +797,8 @@
         r.d_attn[i, mine, :] = grad.astype(bf16)
         attn_copies.append(ship(r.d_attn.at[i, mine, :], r.d_attn.at[i, mine, :], core))
         ffn_part = ffn_part + jnp.sum(mid * value, axis=0, keepdims=True)
-        mix = mixer.total(i, 1)
-        r.out_half[i] = (value + mix).astype(bf16)
-        r.hidden[i] = grad
-    d_hidden = r.hidden
+        r.d_hidden[i] = grad
+    act_line.take(act_line.order[0])
     arrive(attn_copies)
 
     @pl.loop(0, nb)
@@ -750,35 +809,33 @@
 
     heads_sum = net.reduce(r.pq, r.gq)
 
-    drain(wd_copies + wg_copies + wu_copies)
-    gu_sum.finish()
-
-    def to_a(source, target):
-        return [ship(source.at[p["a"]], target.at[k], p) for k, p in enumerate(a_peers)]
-
-    def expert_grad(j, left, target):
-        @pl.loop(0, experts)
-        def _(e):
-            for i in range(nb):
-                r.pkv[0, i * tok : (i + 1) * tok, :] = expand(j, i, e)
-            grad = dot(left[...].reshape(col, part), r.pkv[0], TN).astype(bf16)
-            lane = pl.ds(pl.multiple_of(e * ff, ff), ff)
-            for k in range(na):
-                target[k, :, lane] = grad[k * sub : (k + 1) * sub, :]
-
-    expert_grad(0, r.cotc, r.wd)
-    pending = to_a(r.wd, r.down_in)
-    results = [move(r.wd.at[a], r.down_own)]
+    expert_grad(2, r.scaled, r.wu)
     heads_sum.inner()
+
+    act_line.take(act_line.order[1])
+    act_line.take(act_line.order[2])
+
+    @pl.loop(0, nb)
+    def _(i):
+        total = 0.0
+        for e in range(experts):
+            r.pkv[1, 0:tok, :] = expand(0, i, e)
+            piece = r.wd[:, :, e * ff : (e + 1) * ff].reshape(part, ff)
+            total = total + dot(r.pkv[1, 0:tok, :], piece, NT)
+        mixer.put(i, 1, total, 1)
+        mixer.onward(i, 1, 1)
+
     term = dot(r.d_attn[...].reshape(col, part), r.ho[...], TN).astype(bf16)
     r.gout[...] = term.reshape(na, sub, width)
+    pending += to_a(r.gout, r.gout_in)
     extra = 0.0
     for i in range(nb):
         d_log = jnp.where(which16 < experts, r.late_small[i], 0.0).astype(bf16)
         extra = extra + dot(d_log, r.scaled[i])
     which_row = lax.broadcasted_iota(jnp.int32, (16, part), 0)
     r.extra_own[...] = jnp.where(which_row == experts + 1, ffn_part, extra)
-    expert_grad(1, r.scaled, r.wg)
+    for i in range(nb):
+        r.out_half[i] = (r.hidden[i] + mixer.total(i, 1)).astype(bf16)
     heads_sum.wait()
     out_copies = [
         ship(r.out_half.at[p["b"]], r.block_out.at[mine, own_lane], p) for p in b_peers
@@ -796,10 +853,10 @@
         r.stat[rows, 4:5] = delta
 
     def attend_back(block, first, last, start, stop):
-        @pl.loop(start, stop)
+        @pl.loop(start // deep, stop // deep)
         def _(i):
-            rows = rows_of(i)
-            columns = r.ids[i]
+            rows = deep_rows(i)
+            columns = deep_ids(i)
             query, cot = r.q_rot[rows, :], r.pq[b, rows, :]
             keys, values = r.kv[block, :, :head], r.kv[block, :, head:]
             scores = dot(query, keys, NT) * scale
@@ -838,8 +895,8 @@
         attend_back(lax.rem(a + k, na), k == 1, False, 0, nb)
         r.dkv_send[k - 1] = r.dkv_acc[...].astype(bf16)
         kv_back.append(ship(r.dkv_send.at[k - 1], r.dkv_in.at[k - 1], a_peers[k - 1]))
-    pending += to_a(r.wg, r.gate_in) + to_a(r.gout, r.gout_in)
-    results.append(move(r.wg.at[a], r.gate_own))
+    pending += to_a(r.wu, r.up_in)
+    results.append(move(r.wu.at[a], r.up_own))
     q_lines = []
     for s in range(2):
         attend_back(a, na == 1, True, s * (nb // 2), (s + 1) * (nb // 2))
@@ -852,9 +909,8 @@
         copy.wait_recv()
         out_more.append(ship(r.block_out.at[mine, lane], r.block_out.at[mine, lane], core))
     out_more.append(ship(r.block_out.at[mine, own_lane], r.block_out.at[mine, own_lane], core))
-    expert_grad(2, r.scaled, r.wu)
-    pending += to_a(r.wu, r.up_in)
-    results.append(move(r.wu.at[a], r.up_own))
+    for line in q_lines:
+        line.take(line.order[0])
     arrive(kv_back)
 
     @pl.loop(0, nb)
@@ -875,16 +931,14 @@
             grad * source + value_grad * r.raw[rows, 2 * head :], axis=1, keepdims=True
         )
 
-    def kv_half(s):
-        start, size = cuts[s] * tok, (cuts[s + 1] - cuts[s]) * tok
+    def kv_piece(s):
         return net.spread(
-            lambda i: head_block(r.wide.at[1], i, start, size),
-            lambda i: head_block(r.wide.at[2], i, start, size),
+            lambda i: head_block(r.wide.at[1], i, s * tok, tok),
+            lambda i: head_block(r.wide.at[2], i, s * tok, tok),
+            start=s == 0,
         )
 
-    for line in q_lines:
-        line.take(line.order[0])
-    kv_lines = [kv_half(0)]
+    kv_lines = [kv_piece(s) for s in range(nb)]
     place16 = (b * 2 + y) * 2 + c
     r.s4[place16] = transpose_columns([r.stat[i * tok : (i + 1) * tok, 3:4] for i in range(nb)], tok)
     r.s4[place16, 4:6, 0:head] = r.gain_acc[0:2, :]
@@ -895,29 +949,27 @@
         r.gsend[j] = grad.reshape(na, sub, width)
         return to_a(r.gsend.at[j], r.gin_w.at[j])
 
+    expert_grad(0, r.cotc, r.wd)
+    pending += to_a(r.wd, r.down_in)
+    results.append(move(r.wd.at[a], r.down_own))
     for line in q_lines:
         line.take(line.order[1])
         line.take(line.order[2])
     pending += weight_grad(0)
-    kv_lines[0].take(kv_lines[0].order[0])
-    kv_lines.append(kv_half(1))
-
     mixer_in = TwoLevel(net, r.acc, r.sendc, r.recvc, r.sendy, r.recvy, 1)
     mixer.finish()
     arrive(s4_copies)
-    for s in range(2):
-        if s == 0:
-            kv_lines[0].take(kv_lines[0].order[1])
-            kv_lines[0].take(kv_lines[0].order[2])
+    for i in range(nb):
+        if i < nb - 1:
+            kv_lines[i + 1].after(kv_lines[i])
         else:
-            kv_lines[1].take_all()
-        for i in range(cuts[s], cuts[s + 1]):
-            rows = slice(i * tok, (i + 1) * tok)
-            term = dot(r.wide[0, rows, :], weight(0), NT)
-            term = term + dot(r.wide[1, rows, :], weight(1), NT)
-            mixer_in.put(i, 0, term + dot(r.wide[2, rows, :], weight(2), NT), i)
-        for i in range(cuts[s], cuts[s + 1]):
-            mixer_in.onward(i, 0, i)
+            kv_lines[i].take(kv_lines[i].order[0])
+        kv_lines[i].take(kv_lines[i].order[1])
+        kv_lines[i].take(kv_lines[i].order[2])
+        rows = slice(i * tok, (i + 1) * tok)
+        term = dot(r.wide[0, rows, :], weight(0), NT) + dot(r.wide[1, rows, :], weight(1), NT)
+        mixer_in.put(i, 0, term + dot(r.wide[2, rows, :], weight(2), NT), i)
+        mixer_in.onward(i, 0, i)
     sums = r.s4[0]
     for k in range(1, 4 * nb):
         sums = sums + r.s4[k]
@@ -946,7 +998,7 @@
         )
         x = r.xc[i, mine, :].astype(f32)
         scaled = d_in * r_col
-        grad = d_hidden[i] + scaled * gain_in - x * (r_col * r_col * inner / model)
+        grad = r.d_hidden[i] + scaled * gain_in - x * (r_col * r_col * inner / model)
         attn_part = attn_part + jnp.sum(scaled * x, axis=0, keepdims=True)
         r.out_half[i] = grad.astype(bf16)
 
@@ -997,7 +1049,7 @@
     arrive(in_more)
     results.append(move(r.gin, r.in_rows))
     mixer_in.finish()
-    for line in [heads_sum, pay_line] + cd_sums + ho_lines + q_lines + kv_lines:
+    for line in [heads_sum, pay_line, act_line] + cd_sums + ho_lines + q_lines + kv_lines:
         line.finish()
     for d in range(nb):
 
@@ -1065,6 +1117,7 @@
         sendy=((nb, half, 2 * part), bf16),
         recvy=((nb, half, 2 * part), bf16),
         hidden=((nb, half, part), f32),
+        d_hidden=((nb, half, part), f32),
         scaled=((nb, tok, part), bf16),
         small=((nb, 16, tok), f32),
         small_in=((nb, 16, tok), f32),
@@ -1094,7 +1147,7 @@
         docs=((na, 1, col), f32),
         proj=((4, sub, width), f32),
     )
-    count = 160 + 26 * na
+    count = 224 + 28 * na
     scratch = [pltpu.VMEM(*work[name]) for name in WORK[:-3]] + [
         pltpu.SemaphoreType.DMA((count,)),
         pltpu.SemaphoreType.DMA((count,)),
@@ -1209,7 +1262,7 @@
         dims,
         [
             tokens_in, cotangent, w_query, w_key, w_value, w_output, w_gate, w_up, w_down,
-            expert_ids.T, doc_ids[None], w_router.T, attn_gain[None], ffn_gain[None], q_gain[None],
+            expert_ids.T, doc_ids[None], w_router.T, attn_gain, ffn_gain, q_gain[None],
             k_gain[None], jnp.asarray(speed, f32)[None],
         ],
     )

time: 357 us -> 341 us (0.955)
  Pallas kernels: 354 us -> 340 us
    pallas_call x1, Pallas kernels: 345 us -> 331 us  [layer(): pl.pallas_call(functools.partial(layer_kernel, sizes, dims), out_shape=ou...]
where the time goes in v3:
time: 341 us
  Pallas kernels  340 us (100%)
    pallas_call x1, Pallas kernels, layer(): pl.pallas_call(functools.partial(layer_kernel, sizes, dims), out_shape=ou...  331 us
    pallas_call x1, Pallas kernels, last(): pl.pallas_call(functools.partial(last_kernel, experts, ff, sub), grid=(st...  9.15 us

profile of v3, /device:TPU:0, one launch (start us, length us, event | category | flops | bytes accessed | tf_op | source)
XLA Modules:
  0.0 340.6 jit_solution(8939309389008887047)
XLA Ops:
  0.7 330.6 %layer.1 = (bf16[256,2048]{1,0:T(8,128)(2,1)}, bf16[256,2048]{1,0:T(8,128)(2,1)}, bf16[256,2048]{1,0:T(8,128)(2,1)}, bf16[256,2048]{1,0:T(8,128)(2,1)}, bf16[256...) custom-call(bf16[256,2048]{1,0:T(8,128)(2,1)} %refs_0_.1, ...), custom_call_target="tpu_custom_call" | custom-call | tf_op jit(solution)/shard_map/layer/pallas_call | solution.py:1156
  331.3 9.1 %last.1 = (bf16[256,2048]{1,0:T(8,128)(2,1)}, f32[256,2048]{1,0:T(8,128)}, f32[256,8,256]{2,1,0:T(8,128)}, f32[256,8,256]{2,1,0:T(8,128)}, f32[256,8,256]{2,1,0:...) custom-call(bf16[256,2048]{1,0:T(8,128)(2,1)} %get-tuple-element.38., ...), custom_call_target="tpu_custom_call" | custom-call | tf_op jit(solution)/shard_map/last/pallas_call | solution.py:1213
